TPU v7x, 32 devices: a whole 2x2x4 slice. The times are simulated.
32 devices in a mesh: dp: 32 (over z, y, x, core).
Axes of the slice: x: 2, y: 2, z: 4, core: 2. Of those that a mesh axis runs over, the one named last changes fastest.
Arguments:
- grad_embed: bfloat16 [32, 4000, 2304], P('dp')
- grad_q: bfloat16 [32, 6, 2304, 32], P('dp')
- grad_k: bfloat16 [32, 6, 2304, 16], P('dp')
- grad_v: bfloat16 [32, 6, 2304, 16], P('dp')
- grad_out: bfloat16 [32, 6, 32, 2304], P('dp')
- grad_gate: bfloat16 [32, 6, 2304, 144], P('dp')
- grad_up: bfloat16 [32, 6, 2304, 144], P('dp')
- grad_down: bfloat16 [32, 6, 144, 2304], P('dp')
- grad_norms: bfloat16 [32, 6, 4, 2304], P('dp')
- grad_qk_norms: bfloat16 [32, 6, 2, 256], P('dp')
- first_moment: float32 [16573440], P('dp')
- second_moment: float32 [16573440], P('dp')
- master_param: float32 [16573440], P('dp')
- hyper_params: float32 [5], replicated
Outputs:
- output 1: bfloat16 [4000, 2304], replicated
- output 2: bfloat16 [6, 2304, 32], replicated
- output 3: bfloat16 [6, 2304, 16], replicated
- output 4: bfloat16 [6, 2304, 16], replicated
- output 5: bfloat16 [6, 32, 2304], replicated
- output 6: bfloat16 [6, 2304, 144], replicated
- output 7: bfloat16 [6, 2304, 144], replicated
- output 8: bfloat16 [6, 144, 2304], replicated
- output 9: bfloat16 [6, 4, 2304], replicated
- output 10: bfloat16 [6, 2, 256], replicated
- output 11: float32 [16573440], P('dp')
- output 12: float32 [16573440], P('dp')
- output 13: float32 [16573440], P('dp')
All inputs are finite; a program needn't handle non-finite values.
Results may differ from a plain program's by a relative error of at most 0.001.
Values are sent between devices in bfloat16 or wider.
A program may use at most 1 GiB of HBM per device.

v0:
```python
import math
import jax
import jax.numpy as jnp
from jax import lax
from jax.sharding import PartitionSpec as P

ADAM_STEP = 7
ADAM_EPS = 1e-8
CLIP_EPS = 1e-6
GRAD_COUNT = 10
NORM_COUNT = 2


def adam_step(grad_part, first_part, second_part, master_part, hyper_params, clip_scale, keep_decay):
    learn_rate = hyper_params[0]
    beta_one = hyper_params[1]
    beta_two = hyper_params[2]
    weight_decay = hyper_params[3]
    clipped = grad_part * clip_scale
    moment_one = beta_one * first_part + (1.0 - beta_one) * clipped
    moment_two = beta_two * second_part + (1.0 - beta_two) * (clipped * clipped)
    m_hat = moment_one / (1.0 - beta_one ** ADAM_STEP)
    v_hat = moment_two / (1.0 - beta_two ** ADAM_STEP)
    direction = m_hat / (jnp.sqrt(v_hat) + ADAM_EPS) + jnp.where(keep_decay, weight_decay * master_part, 0.0)
    new_master = master_part - learn_rate * direction
    return moment_one, moment_two, new_master


def split_params(joined, shapes):
    pieces = []
    start_pos = 0
    for tensor_dims in shapes:
        tensor_size = math.prod(tensor_dims)
        pieces.append(joined[start_pos:start_pos + tensor_size].reshape(tensor_dims))
        start_pos = start_pos + tensor_size
    return pieces


def solution(mesh):
    group_size = mesh.shape["dp"]

    def local_update(*arrays):
        grads = arrays[:GRAD_COUNT]
        first_part, second_part, master_part, hyper_params = arrays[GRAD_COUNT:]
        shapes = [grad_arr.shape[1:] for grad_arr in grads]
        sizes = [math.prod(tensor_dims) for tensor_dims in shapes]
        total_len = sum(sizes)
        shard_len = total_len // group_size
        decay_len = total_len - sum(sizes[GRAD_COUNT - NORM_COUNT:])
        local_vec = jnp.concatenate([grad_arr.reshape(-1) for grad_arr in grads]).reshape(group_size, shard_len)
        received = lax.all_to_all(local_vec, "dp", 0, 0, tiled=True)
        grad_part = jnp.sum(received, axis=0, dtype=jnp.float32) / group_size
        square_sum = lax.psum(jnp.sum(grad_part * grad_part), "dp")
        clip_scale = jnp.minimum(1.0, hyper_params[4] / (jnp.sqrt(square_sum) + CLIP_EPS))
        offset = lax.axis_index("dp") * shard_len
        keep_decay = offset + lax.broadcasted_iota(jnp.int32, (shard_len,), 0) < decay_len
        moment_one, moment_two, new_master = adam_step(grad_part, first_part, second_part, master_part, hyper_params, clip_scale, keep_decay)
        full_vec = lax.all_gather(new_master.astype(jnp.bfloat16), "dp", tiled=True)
        return tuple(split_params(full_vec, shapes)) + (moment_one, moment_two, new_master)

    in_specs = tuple([P("dp")] * GRAD_COUNT + [P("dp"), P("dp"), P("dp"), P()])
    out_specs = tuple([P()] * GRAD_COUNT + [P("dp"), P("dp"), P("dp")])
    return jax.shard_map(local_update, mesh=mesh, in_specs=in_specs, out_specs=out_specs, check_vma=False)
```

profile of v0, /device:TPU:3, one launch (start us, length us, event | category | flops | bytes accessed | tf_op | source)
XLA Modules:
  0.0 2288.9 jit_solution(8654406812740228309)
XLA Ops:
  7.2 34.0 %reshape.97 = bf16[9216000]{0:T(1024)(128)(2,1)} reshape(bf16[1,4000,2304]{2,1,0:T(8,128)(2,1)} %param.14) | data formatting | bytes 36864000 | tf_op jit(solution)/shard_map/reshape | solution.py:50
  41.2 16.2 constant_dynamic-update-slice_fusion.9
  85.2 13.7 reshape.102
  107.1 14.1 reshape.103
  121.3 8.5 reshape.104
  144.1 289.7 %while.1 = (u32[]{:T(128)}, bf16[16573440]{0:T(1024)(128)(2,1)}, bf16[32,1,517920]{2,1,0:T(2,128)(2,1)}, u32[]{}, u32[]{}, /*index=5*/u32[]{}) while((u32[]{:T(128)}, bf16[16573440]{0:T(1024)(128)(2,1)}, bf16[32,1,517920]{2,1,0:T(2,128)(2,1)}, u32[]{}, u32[]{}, /*index=5*/u32[]{}) %tuple.32), condition=%wide.cond, body=%wide.body.sunk | while | flops 9 | bytes 16575141
  190.0 8.4 constant_dynamic-update-slice_fusion.12
  208.2 8.4 constant_dynamic-update-slice_fusion.12
  298.7 8.4 constant_dynamic-update-slice_fusion.12
  434.3 196.9 %reduce.1 = bf16[32,517920]{1,0:T(8,128)(2,1)} reduce(bf16[32,1,517920]{2,1,0:T(2,128)(2,1)} %get-tuple-element.43, bf16[]{:T(256)} %broadcast.3), dimensions={1}, to_apply=%get-tuple-element.43.reduce_sub_computation | reduce | bytes 66293760 | tf_op jit(solution)/shard_map/all_to_all | solution.py:51
  631.2 56.1 %reshape.119 = bf16[32,2,258960]{2,1,0:T(2,128)(2,1)} reshape(bf16[32,517920]{1,0:T(8,128)(2,1)} %reduce.1) | data formatting | bytes 66293760
  699.6 713.3 %all-to-all-done = bf16[32,2,258960]{2,1,0:T(2,128)(2,1)} async-done(((bf16[32,2,258960]{2,1,0:T(2,128)(2,1)}), bf16[32,2,258960]{2,1,0:T(2,128)(2,1)}, u32[]{:S(2)}, u32[]{:S(2)}) %all-to-all-start) | async-done | bytes 33146912 | tf_op jit(solution)/shard_map/all_to_all | solution.py:51
  1412.9 75.9 %reshape.120 = bf16[32,1,517920]{2,1,0:T(2,128)(2,1)} reshape(bf16[32,2,258960]{2,1,0:T(2,128)(2,1)} %all-to-all-done) | data formatting | bytes 66293760
  1488.8 77.6 %convert_reduce_fusion = f32[517920]{0:T(1024)S(1)} fusion(bf16[32,1,517920]{2,1,0:T(2,128)(2,1)} %reshape.120), kind=kLoop, calls=%fused_computation | loop fusion | flops 32628960 | bytes 35218560 | tf_op jit(solution)/shard_map/reduce_sum | solution.py:52
  1567.5 43.9 %psum.7 = f32[]{:T(128)} all-reduce(f32[]{:T(128)} %multiply_reduce_fusion), channel_id=1, replica_groups=mesh['dp'=32] {'dp'}, use_global_device_ids=true, to_apply=%region_2.0 | all-reduce | flops 1 | bytes 8 | tf_op jit(solution)/shard_map/psum | solution.py:53
  1612.7 9.4 fusion
  1622.1 10.8 broadcast.2
  1632.9 16.3 dynamic-update-slice
  1649.2 495.7 %all-reduce.3.cloned.1.call-done = bf16[16573440]{0:T(1024)(128)(2,1)} async-done(((bf16[16573440]{0:T(1024)(128)(2,1)}), bf16[16573440]{0:T(1024)(128)(2,1)}) %all-reduce.3.cloned.1.call-update) | async-done | bytes 33146896
  2144.9 8.6 fusion.1
  2153.5 13.3 reshape.112
  2175.1 13.3 reshape.113
  2230.6 16.2 slice.71
  2246.8 33.6 %reshape.107 = bf16[4000,2304]{1,0:T(8,128)(2,1)} reshape(bf16[9216000]{0:T(1024)(128)(2,1)} %slice.71) | data formatting | bytes 36864000 | tf_op jit(solution)/shard_map/reshape | solution.py:34
  (108 shorter events, 375.1 us)
Async XLA Ops:
  121.2 8.5 copy-start.6
  121.2 8.6 copy-start.8
  121.2 8.6 copy-start.3
  121.2 9.6 copy-start.4
  121.2 10.4 copy-start.5
  129.9 3.6 copy-start.1
  133.5 3.6 copy-start.2
  137.1 3.6 copy-start
  687.3 6.5 copy-start.7
  687.3 725.6 %all-to-all-start = ((bf16[32,2,258960]{2,1,0:T(2,128)(2,1)}), bf16[32,2,258960]{2,1,0:T(2,128)(2,1)}, u32[]{:S(2)}, u32[]{:S(2)}) async-start(bf16[32,2,258960]{2,1,0:T(2,128)(2,1)} %reshape.119), calls=%async_computation | async-start | bytes 66322432 | tf_op jit(solution)/shard_map/all_to_all | solution.py:51
  693.7 1451.2 %all-reduce.3.cloned.1.call-start = ((), (), s32[]{:S(2)}) async-start(), calls=%async_computation.1 | async-start | bytes 66293760
  2246.8 33.6 %slice-start = ((bf16[16573440]{0:T(1024)(128)(2,1)}), bf16[55296]{0:T(1024)(128)(2,1)S(1)}, s32[]{:S(2)}) async-start(bf16[16573440]{0:T(1024)(128)(2,1)} %all-reduce.3.cloned.1.call-done), calls=%async_computation.2 | async-start | bytes 221184 | tf_op jit(solution)/shard_map/slice | solution.py:34
  2246.8 34.3 %slice-start.1 = ((bf16[16573440]{0:T(1024)(128)(2,1)}), bf16[3072]{0:T(1024)(128)(2,1)S(1)}, s32[]{:S(2)}) async-start(bf16[16573440]{0:T(1024)(128)(2,1)} %all-reduce.3.cloned.1.call-done), calls=%async_computation.3 | async-start | bytes 12288 | tf_op jit(solution)/shard_map/slice | solution.py:34
Sparse Core Ops, SparseCore 0:
  1649.3 495.4 all-reduce.2
where the time goes:
time: 2310 us; the launch traced here: 2290 us
  waiting for transfers between devices  1210 us (52%)
  local copies, waits for them, and re-layouts  723 us (31%)
  other arithmetic  285 us (12%)
  blocking collectives  43.9 us (2%)
    all_to_all x1, waiting for transfers between devices, local_update(): received = lax.all_to_all(local_vec, 'dp', 0, 0, tiled=True)  713 us
    unnamed x90, local copies, waits for them, and re-layouts  527 us
    unnamed x2, waiting for transfers between devices  496 us
    all_to_all x1, other arithmetic, local_update(): received = lax.all_to_all(local_vec, 'dp', 0, 0, tiled=True)  197 us
    reshape x9, local copies, waits for them, and re-layouts, split_params(): joined[start_pos:start_pos + tensor_size].reshape(tensor_dims)  83.2 us
    reshape x9, local copies, waits for them, and re-layouts, local_update(): grad_arr.reshape(-1)  81.2 us
    reduce_sum x1, other arithmetic, local_update(): grad_part = jnp.sum(received, axis=0, dtype=jnp.float32) / group_size  77.6 us
  transfers between devices with their start and end apart: 2, of which 2 were waited for; matrix products, arithmetic and copies ran while one was open for 0% of the time, Pallas kernels for 0%

commit v1 on v0

v1 whole, which is shorter than its diff:
```python
import math
import jax
import jax.numpy as jnp
from jax import lax
from jax.sharding import PartitionSpec as P
from jax.experimental import pallas as pl
from jax.experimental.pallas import tpu as pltpu

ADAM_STEP = 7
ADAM_EPS = 1e-8
CLIP_EPS = 1e-6

SUB, LANES = 8, 128
TILES = 18
HALF = TILES // 2
ROWS = TILES * SUB
UNIT = ROWS * LANES
WIDTH = TILES * LANES
LAYERS = 6
DEVICES = 32
SHARD = 517920
NORM_LEN = 58368
TAIL = (TILES, SUB, LANES)
STARTS = (0, 500, 524, 536, 548, 572, 680, 788, 896, 900)
EMBED, Q, K, V, OUT, GATE, UP, DOWN, NORMS, END = STARTS
TENSORS = len(STARTS) - 1
COVER = 30
GATHER = 29
HALO = 2 * ROWS
OWN_ROWS = 4048
OWN_BLOCK = 176
FLAT_ROWS = COVER * ROWS
LINE = 4
SHIFTED = {17: 476, 18: 504}


def first_units():
    firsts = [SHIFTED.get(r, (r * SHARD) // UNIT) for r in range(DEVICES)]
    return firsts + [END]


FIRST = first_units()
COVER_FIRST = [min(first, END - COVER) for first in FIRST]
ANY = pl.BlockSpec(memory_space=pl.ANY)
IN_VMEM = pl.BlockSpec(memory_space=pltpu.VMEM)
IN_SMEM = pl.BlockSpec(memory_space=pltpu.SMEM)
BIG_VMEM = 66_000_000


def first_unit(r):
    value = r * (SHARD // math.gcd(SHARD, UNIT)) // (UNIT // math.gcd(SHARD, UNIT))
    for device, first in SHIFTED.items():
        value = jnp.where(r == device, first, value)
    return jnp.where(r == DEVICES, END, value)


def unit_runs(start, stop):
    runs = []
    for tensor in range(TENSORS):
        low, high = max(start, STARTS[tensor]), min(stop, STARTS[tensor + 1])
        if low < high:
            runs.append((tensor, low - STARTS[tensor], high - low, low - start))
    return runs


def tile_copies(refs, runs, slot_ref):
    pairs = []
    for tensor, first, count, slot in runs:
        ref = refs[tensor]
        kind = STARTS[tensor]
        if kind in (EMBED, OUT, DOWN, NORMS):
            pairs.append((ref.at[pl.ds(first, count)], slot_ref.at[pl.ds(slot, count)]))
        elif kind in (GATE, UP):
            for k in range(count):
                layer, col = divmod(first + k, TILES)
                pairs.append((ref.at[layer, :, col], slot_ref.at[slot + k]))
        else:
            step = 2 if kind == Q else 1
            for k in range(0, count, step):
                layer, half = divmod((first + k) // step, 2)
                for row in range(2 * step):
                    part = slot_ref.at[slot + k + row // 2, pl.ds(HALF * (row % 2), HALF)]
                    pairs.append((ref.at[layer, row, pl.ds(HALF * half, HALF)], part))
    return pairs

SLOTS = 8


def pack_kernel(*args):
    refs, (out_ref, stage, in_sem, out_sem) = args[:TENSORS], args[TENSORS:]
    depth = stage.shape[0]

    def start_in(r):
        slot = r % depth
        if r >= depth:
            pltpu.make_async_copy(stage.at[slot], out_ref.at[r - depth], out_sem.at[slot]).wait()
        for src, dst in tile_copies(refs, unit_runs(COVER_FIRST[r], COVER_FIRST[r] + COVER), stage.at[slot]):
            pltpu.make_async_copy(src, dst, in_sem.at[slot]).start()

    ahead = depth // 2
    for r in range(ahead):
        start_in(r)
    for r in range(DEVICES):
        if r + ahead < DEVICES:
            start_in(r + ahead)
        slot = r % depth
        pltpu.make_async_copy(out_ref.at[r], stage.at[slot], in_sem.at[slot]).wait()
        pltpu.make_async_copy(stage.at[slot], out_ref.at[r], out_sem.at[slot]).start()
    for r in range(DEVICES - depth, DEVICES):
        slot = r % depth
        pltpu.make_async_copy(stage.at[slot], out_ref.at[r], out_sem.at[slot]).wait()


def pack(tensors):
    return pl.pallas_call(
        pack_kernel,
        name="pack",
        out_shape=jax.ShapeDtypeStruct((DEVICES, COVER) + TAIL, jnp.bfloat16),
        in_specs=[ANY] * TENSORS,
        out_specs=ANY,
        scratch_shapes=[
            pltpu.VMEM((SLOTS, COVER) + TAIL, jnp.bfloat16),
            pltpu.SemaphoreType.DMA((SLOTS,)),
            pltpu.SemaphoreType.DMA((SLOTS,)),
        ],
        compiler_params=pltpu.CompilerParams(vmem_limit_bytes=BIG_VMEM),
    )(*tensors)


def unpack_kernel(*args):
    gathered, outs, (stage, in_sem, out_sem) = args[0], args[1:-3], args[-3:]
    depth = stage.shape[0]

    def wait_out(r):
        slot = r % depth
        count = FIRST[r + 1] - FIRST[r]
        part = stage.at[slot, pl.ds(0, count)]
        pltpu.make_async_copy(part, gathered.at[r, pl.ds(0, count)], out_sem.at[slot]).wait()

    def start_in(r):
        slot = r % depth
        if r >= depth:
            wait_out(r - depth)
        pltpu.make_async_copy(gathered.at[r], stage.at[slot], in_sem.at[slot]).start()

    ahead = depth // 2
    for r in range(ahead):
        start_in(r)
    for r in range(DEVICES):
        if r + ahead < DEVICES:
            start_in(r + ahead)
        slot = r % depth
        pltpu.make_async_copy(gathered.at[r], stage.at[slot], in_sem.at[slot]).wait()
        for dst, src in tile_copies(outs, unit_runs(FIRST[r], FIRST[r + 1]), stage.at[slot]):
            pltpu.make_async_copy(src, dst, out_sem.at[slot]).start()
    for r in range(DEVICES - depth, DEVICES):
        wait_out(r)


def unpack(gathered, tensor_shapes):
    return pl.pallas_call(
        unpack_kernel,
        name="unpack",
        out_shape=[jax.ShapeDtypeStruct(dims, jnp.bfloat16) for dims in tensor_shapes],
        in_specs=[ANY],
        out_specs=[ANY] * TENSORS,
        scratch_shapes=[
            pltpu.VMEM((SLOTS, GATHER) + TAIL, jnp.bfloat16),
            pltpu.SemaphoreType.DMA((SLOTS,)),
            pltpu.SemaphoreType.DMA((SLOTS,)),
        ],
        compiler_params=pltpu.CompilerParams(vmem_limit_bytes=BIG_VMEM),
    )(gathered)


def place():
    me = lax.axis_index("dp")
    return me // 8, (me // 4) % 2, (me // 2) % 2, me % 2


def index_of(z, y, x, c):
    return ((z * 2 + y) * 2 + x) * 2 + c


def greet(peers):
    barrier = pltpu.get_barrier_semaphore()
    for peer in peers:
        pl.semaphore_signal(barrier, inc=1, device_id=(peer,), device_id_type=pl.DeviceIdType.MESH)
    pl.semaphore_wait(barrier, len(peers))


def remote(src, dst, send, recv, peer):
    return pltpu.make_async_remote_copy(src_ref=src, dst_ref=dst, send_sem=send, recv_sem=recv, device_id=(peer,), device_id_type=pl.DeviceIdType.MESH)


class Sems:
    def __init__(self, send, recv):
        self.send, self.recv, self.used = send, recv, 0

    def copy(self, src, dst, peer):
        k = self.used
        self.used += 1
        return remote(src, dst, self.send.at[k], self.recv.at[k], peer)


COLORS = range(4)
OUTER = 7


def jobs_of(sizes, first=0):
    steps = [[] for _ in sizes[0]]
    for color in COLORS:
        for step, count in enumerate(sizes[color]):
            if count:
                steps[step].append((color, first, count))
                first += count
    return steps


RS_WIDE, RS_THIN = (1,) * 10, (1, 0) * 5
RS_STEPS = jobs_of((RS_WIDE, RS_WIDE, RS_THIN, RS_THIN))


class Reduce:
    def __init__(self, job, x_ref, g_ref, own, sum1, own_sem, sum_slot, got1, got2, got3, send, recv):
        self.color, self.first, self.count = job
        self.units = pl.ds(self.first, self.count)
        self.g_ref = g_ref
        z, y, x, c = place()
        self.z = z
        self.late = self.color >= 2
        by_x = self.color % 2 == 0
        self.mine = y if by_x else x
        if by_x:
            group = ((y, 1 - x, c), (y, 1 - x, 1 - c), (y, x, 1 - c))
            side = index_of(z, 1 - y, x, c)
            part = lambda yy, xx, cc: x_ref.at[:, :, xx, cc, self.units]
        else:
            group = ((1 - y, x, c), (1 - y, x, 1 - c), (y, x, 1 - c))
            side = index_of(z, y, 1 - x, c)
            part = lambda yy, xx, cc: x_ref.at[:, yy, :, cc, self.units]
        n = pl.ds(0, self.count)
        self.own = own.at[sum_slot, self.color, :, :, n]
        self.sum1 = sum1.at[sum_slot, self.color, :, :, n]
        self.got1, self.got2, self.got3 = got1, got2, got3
        sems = Sems(send, recv)
        self.copies1 = [sems.copy(part(*who), got1.at[k], index_of(z, *who)) for k, who in enumerate(group)]
        self.own_copy = pltpu.make_async_copy(part(y, x, c), self.own, own_sem.at[sum_slot, self.color])
        others = [(z + k) % LINE for k in range(1, LINE)]
        peers = [index_of(zz, y, x, c) for zz in others]
        if self.late:
            self.copies2 = [sems.copy(self.sum1.at[zz], got2.at[k], peer) for k, (zz, peer) in enumerate(zip(others, peers))]
            self.copies3 = [sems.copy(got2.at[0, 1 - self.mine], got3.at[0], side)]
        else:
            self.copies2 = [sems.copy(self.sum1.at[:, 1 - self.mine], got2, side)]
            self.copies3 = [sems.copy(got2.at[zz], got3.at[k], peer) for k, (zz, peer) in enumerate(zip(others, peers))]

    def add1(self):
        def body(i, carry):
            zz, side, u = i // (2 * self.count), (i // self.count) % 2, i % self.count
            total = self.own[zz, side, u].astype(jnp.float32)
            for k in range(len(self.copies1)):
                total = total + self.got1[k, zz, side, u].astype(jnp.float32)
            self.sum1[zz, side, u] = total
            return carry

        lax.fori_loop(0, 2 * LINE * self.count, body, 0)

    def add2(self):
        def early(i, carry):
            zz, u = i // self.count, i % self.count
            self.got2[zz, u] = self.got2[zz, u] + self.sum1[zz, self.mine, u]
            return carry

        def late(i, carry):
            side, u = i // self.count, i % self.count
            total = self.sum1[self.z, side, u]
            for k in range(LINE - 1):
                total = total + self.got2[k, side, u]
            self.got2[0, side, u] = total
            return carry

        if self.late:
            lax.fori_loop(0, 2 * self.count, late, 0)
        else:
            lax.fori_loop(0, LINE * self.count, early, 0)

    def add3(self, begin, end, acc):
        def body(u, acc):
            total = self.got2[0, self.mine, u] if self.late else self.got2[self.z, u]
            for k in range(len(self.copies3)):
                total = total + self.got3[k, u]
            mean = total * (1.0 / DEVICES)
            slot = self.first + u
            self.g_ref[slot] = mean
            square = jnp.sum(mean * mean, axis=0)
            return acc + jnp.where((slot >= begin) & (slot < end), square, 0.0)

        return lax.fori_loop(0, self.count, body, acc)


def start_all(copies):
    for copy in copies:
        copy.start()


def recv_all(copies):
    for copy in copies:
        copy.wait_recv()


def send_all(copies):
    for copy in copies:
        copy.wait_send()


def reduce_kernel(*args):
    x_ref, g_ref, n_ref, own, sum1, norm_buf, own_sem, send_n, recv_n = args[:9]
    rest = list(args[9:])
    z, y, x, c = place()
    me = lax.axis_index("dp")
    z_peers = [index_of((z + k) % LINE, y, x, c) for k in range(1, LINE)]
    plane = [index_of(z, y, x, 1 - c), index_of(z, y, 1 - x, c), index_of(z, y, 1 - x, 1 - c), index_of(z, 1 - y, x, c), index_of(z, 1 - y, x, 1 - c)]
    greet(plane + z_peers)
    steps = []
    for t, jobs in enumerate(RS_STEPS):
        steps.append([])
        for job in jobs:
            steps[t].append(Reduce(job, x_ref, g_ref, own, sum1, own_sem, t % 2, *rest[:5]))
            rest = rest[5:]
    total_steps = len(steps)

    def start1(t):
        for k in range(3):
            for job in steps[t]:
                job.copies1[k].start()
        for job in steps[t]:
            job.own_copy.start()

    first = first_unit(me)
    begin = first - jnp.minimum(first, END - COVER)
    end = begin + first_unit(me + 1) - first
    acc = jnp.zeros((SUB, LANES), jnp.float32)
    start1(0)
    for t in range(total_steps + 2):
        if t + 1 < total_steps:
            start1(t + 1)
        if t < total_steps:
            for job in steps[t]:
                recv_all(job.copies1)
                job.own_copy.wait()
                if t >= 2:
                    send_all([copy for old in steps[t - 2] if old.color == job.color for copy in old.copies2])
                job.add1()
            for job in steps[t]:
                start_all(job.copies2)
        if 1 <= t <= total_steps:
            for job in steps[t - 1]:
                recv_all(job.copies2)
                job.add2()
            for job in steps[t - 1]:
                start_all(job.copies3)
        if t >= 2:
            for job in steps[t - 2]:
                recv_all(job.copies3)
                acc = job.add3(begin, end, acc)

    sems = Sems(send_n, recv_n)
    sent, used = [], 0
    norm_buf[0] = acc
    for peers in (z_peers, plane[:3], plane[3:4]):
        copies = [sems.copy(norm_buf.at[used], norm_buf.at[used + 1 + k], peer) for k, peer in enumerate(peers)]
        start_all(copies)
        recv_all(copies)
        sent += copies
        total = norm_buf[used]
        for k in range(len(peers)):
            total = total + norm_buf[used + 1 + k]
        used += 1 + len(peers)
        norm_buf[used] = total
    n_ref[0] = jnp.sum(norm_buf[used])

    send_all(sent)
    for t, jobs in enumerate(steps):
        for job in jobs:
            send_all(job.copies1 + job.copies3)
            if not any(later.color == job.color for later in sum(steps[t + 2:t + 3], [])):
                send_all(job.copies2)


def reduce_scatter(packed):
    dma = pltpu.SemaphoreType.DMA
    scratch = []
    largest = max(RS_WIDE)
    for color, first, count in sum(RS_STEPS, []):
        late = color >= 2
        scratch += [
            pltpu.VMEM((3, LINE, 2, count) + TAIL, jnp.bfloat16),
            pltpu.VMEM(((3, 2, count) if late else (LINE, count)) + TAIL, jnp.float32),
            pltpu.VMEM((1 if late else 3, count) + TAIL, jnp.float32),
            dma((OUTER,)),
            dma((OUTER,)),
        ]
    return pl.pallas_call(
        reduce_kernel,
        name="reduce_scatter",
        out_shape=[jax.ShapeDtypeStruct((COVER,) + TAIL, jnp.float32), jax.ShapeDtypeStruct((1,), jnp.float32)],
        in_specs=[ANY],
        out_specs=[IN_VMEM, IN_SMEM],
        scratch_shapes=[
            pltpu.VMEM((2, len(COLORS), LINE, 2, largest) + TAIL, jnp.bfloat16),
            pltpu.VMEM((2, len(COLORS), LINE, 2, largest) + TAIL, jnp.float32),
            pltpu.VMEM((11, SUB, LANES), jnp.float32),
            dma((2, len(COLORS))),
            dma((OUTER,)),
            dma((OUTER,)),
        ] + scratch,
        compiler_params=pltpu.CompilerParams(collective_id=0, has_side_effects=True, vmem_limit_bytes=BIG_VMEM),
    )(packed.reshape((LINE, 2, 2, 2, COVER) + TAIL))


AG_STEPS = jobs_of(((1,) * 10, (1,) * 9 + (0,), (1, 0) * 5, (1, 0) * 5))


class Gather:
    def __init__(self, job, a_ref, b_ref, send, recv):
        color, first, count = job
        u = pl.ds(first, count)
        z, y, x, c = place()
        z_peers = [index_of((z + k) % LINE, y, x, c) for k in range(1, LINE)]
        y_peer, x_peer, c_peer = index_of(z, 1 - y, x, c), index_of(z, y, 1 - x, c), index_of(z, y, x, 1 - c)
        by_x = color % 2 == 0
        side, last = (y_peer, x_peer) if by_x else (x_peer, y_peer)
        sems = Sems(send, recv)
        here, row = b_ref.at[z, y, x, c, u], b_ref.at[:, y, x, c, u]
        pair = b_ref.at[z, :, x, c, u] if by_x else b_ref.at[z, y, :, c, u]
        half = b_ref.at[:, :, x, c, u] if by_x else b_ref.at[:, y, :, c, u]
        full = b_ref.at[:, :, :, c, u]
        if color < 2:
            self.stages = [[sems.copy(a_ref.at[u], here, peer) for peer in z_peers], [sems.copy(row, row, side)]]
        else:
            self.stages = [[sems.copy(a_ref.at[u], here, side)], [sems.copy(pair, pair, peer) for peer in z_peers]]
        self.stages += [[sems.copy(half, half, last)], [sems.copy(full, full, c_peer)]]


def gather_kernel(a_ref, b_ref, own_sem, *rest):
    z, y, x, c = place()
    z_peers = [index_of((z + k) % LINE, y, x, c) for k in range(1, LINE)]
    greet(z_peers + [index_of(z, 1 - y, x, c), index_of(z, y, 1 - x, c), index_of(z, y, x, 1 - c)])
    own = pltpu.make_async_copy(a_ref.at[pl.ds(0, GATHER)], b_ref.at[z, y, x, c], own_sem)
    own.start()
    steps = []
    for jobs in AG_STEPS:
        steps.append([])
        for job in jobs:
            steps[-1].append(Gather(job, a_ref, b_ref, *rest[:2]))
            rest = rest[2:]
    count, stages = len(steps), 4

    def start(t, stage):
        if 0 <= t < count:
            if stage:
                for job in steps[t]:
                    recv_all(job.stages[stage - 1])
                    start_all(job.stages[stage])
            else:
                for job in steps[t]:
                    start_all(job.stages[0])

    start(0, 0)
    start(1, 0)
    own.wait()
    for t in range(count + stages):
        start(t + 2, 0)
        for stage in range(1, stages):
            start(t + 1 - stage, stage)
    for jobs in steps:
        for job in jobs:
            recv_all(job.stages[-1])
            for copies in job.stages:
                send_all(copies)


def all_gather(chunk):
    dma = pltpu.SemaphoreType.DMA
    out = pl.pallas_call(
        gather_kernel,
        name="all_gather",
        out_shape=jax.ShapeDtypeStruct((LINE, 2, 2, 2, GATHER) + TAIL, jnp.bfloat16),
        in_specs=[IN_VMEM],
        out_specs=ANY,
        scratch_shapes=[dma] + [dma((OUTER,))] * (2 * len(sum(AG_STEPS, []))),
        compiler_params=pltpu.CompilerParams(collective_id=1, has_side_effects=True, vmem_limit_bytes=BIG_VMEM),
    )(chunk)
    return out.reshape((DEVICES, GATHER) + TAIL)


def lanes(rows):
    return lax.broadcasted_iota(jnp.int32, (rows, LANES), 1)


def among(u, *starts):
    found = False
    for start in starts:
        stop = STARTS[STARTS.index(start) + 1]
        found = ((u >= start) & (u < stop)) | found
    return found


def rolled(value, shift):
    shift = shift % LANES
    return value if shift == 0 else pltpu.roll(value, shift, 1)


def turned(tiles):
    blank = [jnp.zeros((SUB, LANES), jnp.float32)] * (LANES // SUB - len(tiles))
    return jnp.concatenate(tiles + blank, axis=0).T


def narrow_blocks(width):
    step = LANES // width
    return [(col, min(step, HALF - col)) for col in range(0, HALF, step)]


def tile(ref, unit, index):
    return ref.at[pl.ds(pl.multiple_of(unit * ROWS + index * SUB, SUB), SUB), :]


def narrow_to_flat(in_ref, unit, flat, row, wide, width):
    per, step, lane = width // SUB, LANES // width, lanes(width)
    for col, count in narrow_blocks(width):
        wide[...] = turned([tile(in_ref, unit, HALF * r + col + e)[...] for e in range(count) for r in range(per)])
        for e in range(count):
            value = None
            for j in range(step):
                pick = rolled(wide[pl.ds(j, width, stride=step), :], width * (j - e))
                value = pick if value is None else jnp.where(lane >= width * j, pick, value)
            flat[pl.ds(row + width * (col + e), width), :] = value


def narrow_to_tiles(flat, row, out_ref, unit, wide, width):
    per, step, lane = width // SUB, LANES // width, lanes(width)
    for col, count in narrow_blocks(width):
        for j in range(step):
            value = None
            for e in range(count):
                pick = rolled(flat[pl.ds(row + width * (col + e), width), :], width * (e - j))
                value = pick if value is None else jnp.where(lane >= width * e, pick, value)
            wide[pl.ds(j, width, stride=step), :] = value
        back = wide[...].T
        for e in range(count):
            for r in range(per):
                at = width * e + SUB * r
                index = HALF * r + col + e
                out_ref[unit + index // TILES, index % TILES] = back[at:at + SUB].astype(jnp.bfloat16)


EDGE = ROWS - LANES


def unit_to_flat(in_ref, unit, flat, row, u, wide, tail):
    @pl.when(among(u, EMBED, OUT, DOWN))
    def _():
        for e in range(SUB):
            flat[pl.ds(row + TILES * e, TILES), :] = in_ref[pl.ds(row + e, TILES, stride=SUB), :]

    @pl.when(among(u, NORMS))
    def _():
        flat[pl.ds(row, ROWS), :] = in_ref[pl.ds(row, ROWS), :]

    @pl.when(among(u, K, V))
    def _():
        narrow_to_flat(in_ref, unit, flat, row, wide, EDGE)

    @pl.when(among(u, GATE, UP))
    def _():
        wide[...] = turned([tile(in_ref, unit, t)[...] for t in range(LANES // SUB)])
        tail[...] = turned([tile(in_ref, unit, t)[...] for t in range(LANES // SUB, TILES)])
        lane = lanes(EDGE)
        before = None
        for j in range(SUB):
            head = rolled(wide[pl.ds(j, EDGE, stride=SUB), :], EDGE * j)
            rest = rolled(tail[pl.ds(j, EDGE, stride=SUB), :], EDGE * j)
            flat[pl.ds(row + j, EDGE, stride=HALF), :] = head if before is None else jnp.where(lane < EDGE * j, before, head)
            before = jnp.where((lane >= EDGE * j) & (lane < EDGE * (j + 1)), rest, head)
        flat[pl.ds(row + SUB, EDGE, stride=HALF), :] = before


def unit_to_tiles(flat, row, out_ref, unit, u, wide, tail):
    @pl.when(among(u, EMBED, OUT, DOWN))
    def _():
        for t in range(TILES):
            out_ref[unit, t] = flat[pl.ds(row + t, SUB, stride=TILES), :].astype(jnp.bfloat16)

    @pl.when(among(u, NORMS))
    def _():
        out_ref[unit] = flat[pl.ds(row, ROWS), :].reshape(TAIL).astype(jnp.bfloat16)

    @pl.when(among(u, K, V))
    def _():
        narrow_to_tiles(flat, row, out_ref, unit, wide, EDGE)

    @pl.when(among(u, GATE, UP))
    def _():
        lane = lanes(EDGE)
        for j in range(SUB):
            here = flat[pl.ds(row + j, EDGE, stride=HALF), :]
            after = flat[pl.ds(row + j + 1, EDGE, stride=HALF), :]
            wide[pl.ds(j, EDGE, stride=SUB), :] = rolled(jnp.where(lane >= EDGE * j, here, after), -EDGE * j)
            tail[pl.ds(j, EDGE, stride=SUB), :] = rolled(after, -EDGE * j)
        out_ref[unit, pl.ds(0, LANES // SUB)] = wide[...].T.reshape(LANES // SUB, SUB, LANES).astype(jnp.bfloat16)
        out_ref[unit, pl.ds(LANES // SUB, 2)] = tail[...].T[0:EDGE].reshape(2, SUB, LANES).astype(jnp.bfloat16)


def local_place():
    me = lax.axis_index("dp")
    return me, first_unit(me)


def blocks_of(rows, block, body):
    def step(i, carry):
        body(pl.multiple_of(i * block, SUB))
        return carry

    lax.fori_loop(0, rows // block, step, 0)


def to_flat_kernel(in_ref, out_ref, flat, wide, tail):
    me, first = local_place()
    first = jnp.minimum(first, END - COVER)
    offset = me * SHARD - first * UNIT

    def pair(i, carry):
        unit = 2 * i
        u = first + unit

        @pl.when(among(u, Q))
        def _():
            narrow_to_flat(in_ref, unit, flat, unit * ROWS, wide, 2 * EDGE)

        for j in range(2):
            unit_to_flat(in_ref, unit + j, flat, (unit + j) * ROWS, u + j, wide, tail)
        return carry

    lax.fori_loop(0, COVER // 2, pair, 0)
    flat[pl.ds(FLAT_ROWS, SUB), :] = jnp.zeros((SUB, LANES), jnp.float32)
    row, left = offset // LANES, offset % LANES
    lane = lanes(OWN_BLOCK)
    turn = (LANES - left) % LANES

    def move(k):
        here = flat[pl.ds(row + k, OWN_BLOCK), :]
        after = flat[pl.ds(row + k + 1, OWN_BLOCK), :]
        out_ref[pl.ds(k, OWN_BLOCK), :] = pltpu.roll(jnp.where(lane >= left, here, after), turn, 1)

    blocks_of(OWN_ROWS, OWN_BLOCK, move)


def to_flat(tiles):
    square = pltpu.VMEM((LANES, LANES), jnp.float32)
    return pl.pallas_call(
        to_flat_kernel,
        name="to_flat",
        out_shape=jax.ShapeDtypeStruct((OWN_ROWS, LANES), jnp.float32),
        in_specs=[IN_VMEM],
        out_specs=IN_VMEM,
        scratch_shapes=[pltpu.VMEM((FLAT_ROWS + SUB, LANES), jnp.float32), square, square],
    )(tiles.reshape(FLAT_ROWS, LANES))


def to_tiles_kernel(before_ref, in_ref, out_ref, joined, flat, wide, tail):
    me, first = local_place()
    offset = me * SHARD - first * UNIT
    row, left = offset // LANES, offset % LANES
    lane = lanes(ROWS)

    def fill(ref, base, block):
        def move(k):
            joined[pl.ds(base + k, block), :] = pltpu.roll(ref[pl.ds(k, block), :], left, 1)
        return move

    blocks_of(HALO, ROWS, fill(before_ref, 0, ROWS))
    blocks_of(OWN_ROWS, OWN_BLOCK, fill(in_ref, HALO, OWN_BLOCK))
    joined[pl.ds(HALO + OWN_ROWS, FLAT_ROWS - OWN_ROWS), :] = jnp.zeros((FLAT_ROWS - OWN_ROWS, LANES), jnp.float32)

    def align(k):
        here = joined[pl.ds(HALO - row + k, ROWS), :]
        above = joined[pl.ds(HALO - 1 - row + k, ROWS), :]
        flat[pl.ds(k, ROWS), :] = jnp.where(lane >= left, here, above)

    blocks_of(FLAT_ROWS, ROWS, align)

    def pair(i, carry):
        unit = 2 * i
        u = first + unit

        @pl.when(among(u, Q))
        def _():
            narrow_to_tiles(flat, unit * ROWS, out_ref, unit, wide, 2 * EDGE)

        for j in range(2):
            unit_to_tiles(flat, (unit + j) * ROWS, out_ref, unit + j, u + j, wide, tail)
        return carry

    lax.fori_loop(0, COVER // 2, pair, 0)


def to_tiles(before, share):
    square = pltpu.VMEM((LANES, LANES), jnp.float32)
    return pl.pallas_call(
        to_tiles_kernel,
        name="to_tiles",
        out_shape=jax.ShapeDtypeStruct((COVER,) + TAIL, jnp.bfloat16),
        in_specs=[IN_VMEM, IN_VMEM],
        out_specs=IN_VMEM,
        scratch_shapes=[pltpu.VMEM((HALO + FLAT_ROWS, LANES), jnp.float32), pltpu.VMEM((FLAT_ROWS, LANES), jnp.float32), square, square],
    )(before, share)


def adam_step(grad_part, first_part, second_part, master_part, hyper_params, clip_scale, keep_decay):
    learn_rate, beta_one, beta_two, weight_decay = (hyper_params[k] for k in range(4))
    clipped = grad_part * clip_scale
    moment_one = beta_one * first_part + (1.0 - beta_one) * clipped
    moment_two = beta_two * second_part + (1.0 - beta_two) * (clipped * clipped)
    m_hat = moment_one / (1.0 - beta_one ** ADAM_STEP)
    v_hat = moment_two / (1.0 - beta_two ** ADAM_STEP)
    direction = m_hat / (jnp.sqrt(v_hat) + ADAM_EPS) + jnp.where(keep_decay, weight_decay * master_part, 0.0)
    new_master = master_part - learn_rate * direction
    return moment_one, moment_two, new_master


def row_tiles(mat):
    return mat.reshape(-1, SUB, TILES, LANES).transpose(0, 2, 1, 3)


def from_row_tiles(tiles):
    return tiles.transpose(0, 2, 1, 3).reshape(-1, WIDTH)


def solution(mesh):
    def local_update(*arrays):
        grads, (first_part, second_part, master_part, hyper_params) = arrays[:-4], arrays[-4:]
        me = lax.axis_index("dp")

        def tiles_of(tensor):
            arr, kind = grads[tensor], STARTS[tensor]
            if kind in (EMBED, OUT, DOWN):
                return row_tiles(arr.reshape(-1, WIDTH))
            width = arr.shape[-1]
            tiles = row_tiles(arr.reshape(LAYERS, WIDTH, width).transpose(0, 2, 1).reshape(-1, WIDTH))
            return tiles.reshape((LAYERS, width // SUB) + TAIL)

        tensors = [tiles_of(k) for k in range(TENSORS - 1)]
        blank = jnp.zeros(((END - NORMS) * UNIT - NORM_LEN,), jnp.bfloat16)
        small = jnp.concatenate([arr.reshape(-1) for arr in grads[TENSORS - 1:]] + [blank])
        tensors.append(small.reshape((END - NORMS,) + TAIL))
        grad_tiles, squares = reduce_scatter(pack(tensors))
        clip_scale = jnp.minimum(1.0, hyper_params[4] / (jnp.sqrt(squares[0]) + CLIP_EPS))
        grad_part = to_flat(grad_tiles).reshape(-1)[:SHARD]
        keep_decay = me * SHARD + lax.broadcasted_iota(jnp.int32, (SHARD,), 0) < SHARD * DEVICES - NORM_LEN
        moment_one, moment_two, new_master = adam_step(grad_part, first_part, second_part, master_part, hyper_params, clip_scale, keep_decay)
        before = lax.ppermute(new_master[SHARD - HALO * LANES:], "dp", [(r, r + 1) for r in range(DEVICES - 1)])
        padded = jnp.pad(new_master, (0, OWN_ROWS * LANES - SHARD))
        chunk = to_tiles(before.reshape(HALO, LANES), padded.reshape(OWN_ROWS, LANES))
        outs = unpack(all_gather(chunk), [t.shape for t in tensors])

        def tensor_of(tensor):
            tiles, dims = outs[tensor], grads[tensor].shape[1:]
            if STARTS[tensor] in (EMBED, OUT, DOWN):
                return from_row_tiles(tiles).reshape(dims)
            mat = from_row_tiles(tiles.reshape((-1,) + TAIL))
            return mat.reshape(LAYERS, dims[-1], WIDTH).transpose(0, 2, 1)

        results = [tensor_of(k) for k in range(TENSORS - 1)]
        flat_small, start = outs[-1].reshape(-1), 0
        for arr in grads[TENSORS - 1:]:
            size = math.prod(arr.shape)
            results.append(flat_small[start:start + size].reshape(arr.shape[1:]))
            start += size
        return tuple(results) + (moment_one, moment_two, new_master)

    in_specs = tuple([P("dp")] * 13 + [P()])
    out_specs = tuple([P()] * 10 + [P("dp"), P("dp"), P("dp")])
    return jax.shard_map(local_update, mesh=mesh, in_specs=in_specs, out_specs=out_specs, check_vma=False)
```

time: 2310 us -> 579 us (0.25)
  the two profiles are of different devices: /device:TPU:3 before, /device:TPU:27 now
where the time goes in v1:
time: 579 us; the launch traced here: 578 us
  Pallas kernels  550 us (95%)
  other arithmetic  9.94 us (2%)
  local copies, waits for them, and re-layouts  8.49 us (1%)
  between operations  7.22 us (1%)
    pallas_call x1, Pallas kernels, reduce_scatter(): pl.pallas_call(reduce_kernel, name='reduce_scatter', out_shape=[jax.Shape...  306 us
    pallas_call x1, Pallas kernels, all_gather(): pl.pallas_call(gather_kernel, name='all_gather', out_shape=jax.ShapeDtype...  173 us
    pallas_call x1, Pallas kernels, pack(): pl.pallas_call(pack_kernel, name='pack', out_shape=jax.ShapeDtypeStruct((...  24.1 us
    pallas_call x1, Pallas kernels, unpack(): pl.pallas_call(unpack_kernel, name='unpack', out_shape=[jax.ShapeDtypeStr...  22.9 us
    pallas_call x1, Pallas kernels, to_flat(): pl.pallas_call(to_flat_kernel, name='to_flat', out_shape=jax.ShapeDtypeSt...  12.1 us
  transfers between devices with their start and end apart: 1, of which 1 were waited for; matrix products, arithmetic and copies ran while one was open for 0% of the time, Pallas kernels for 0%

profile of v1, /device:TPU:27, one launch (start us, length us, event | category | flops | bytes accessed | tf_op | source)
XLA Modules:
  0.0 578.1 jit_solution(5724118957186781841)
XLA Ops:
  0.6 1.4 fusion
  7.3 0.7 copy.27
  8.0 0.9 reshape.126
  8.9 0.7 pad_maximum_fusion
  9.6 24.1 %pack.1 = bf16[32,30,18,8,128]{4,3,2,1,0:T(8,128)(2,1)} custom-call(bf16[500,18,8,128]{3,2,1,0:T(8,128)(2,1)} %bitcast.119, bf16[6,4,18,8,128]{4,3,2,1,0:T(8,128)(2,1)} %bitcast.125, bf16[6,2,18,8,128]{4,3,2,1,0:T(8,128)(2,1)} %bitcast.128, bf16[6,2,18,8,128]{4,3,2,1,0:T(8,128)(2,1)} %bitcast.129, bf16[24,18,8,128]{3,2,1,0:T(8,128)(2,1)} %bitcast.126, ...), custom_call_target="tpu_custom_call" | custom-call | tf_op jit(solution)/shard_map/pack/pallas_call | solution.py:115
  33.7 306.2 %reduce_scatter.1 = (f32[30,18,8,128]{3,2,1,0:T(8,128)}, f32[1]{0:T(128)}) custom-call(bf16[4,2,2,2,30,18,8,128]{7,6,5,4,3,2,1,0:T(8,128)(2,1)} %bitcast.117), custom_call_target="tpu_custom_call" | custom-call | tf_op jit(solution)/shard_map/reduce_scatter/pallas_call | solution.py:404
  340.6 0.0 copy-start.1
  340.6 12.1 %to_flat.1 = f32[4048,128]{1,0:T(8,128)} custom-call(f32[4320,128]{1,0:T(8,128)} %bitcast.124), custom_call_target="tpu_custom_call" | custom-call | tf_op jit(solution)/shard_map/to_flat/pallas_call | solution.py:661
  353.4 0.0 copy-done.1
  353.4 9.3 %multiply_subtract_fusion = (f32[517920]{0:T(1024)S(1)}, f32[517920]{0:T(1024)}, f32[517920]{0:T(1024)}) fusion(f32[517920]{0:T(1024)S(1)} %copy-done.1, f32[]{:T(128)} %bitcast.39, s32[]{:T(128)S(6)} %mul.92, f32[]{:T(128)S(6)} %sub.18, f32[]{:T(128)S(6)} %sub.16, f32[]{:T(128)} %bitcast, f32[]{:T(128)} %bitcast.37, f32[518144]{0:T(1024)} %bitcast.120, ...), kind=kLoop, calls=%fused_computation.2 | loop fusion | flops 9840480 | bytes 14501800 | tf_op jit(solution)/shard_map/sub | solution.py:728
  362.7 0.0 copy-start
  362.7 0.1 slice.42
  362.8 1.9 collective-permute-start
  364.7 1.4 pad_bitcast_fusion.in_ref
  366.1 0.0 copy-done
  366.1 0.9 collective-permute-done
  367.1 0.7 copy-done.2
  367.7 11.5 %to_tiles.1.a_ref = bf16[30,18,8,128]{3,2,1,0:T(8,128)(2,1)} custom-call(f32[288,128]{1,0:T(8,128)} %bitcast.130, f32[4048,128]{1,0:T(8,128)} %pad_bitcast_fusion.in_ref), custom_call_target="tpu_custom_call" | custom-call | tf_op jit(solution)/shard_map/to_tiles/pallas_call | solution.py:710
  379.3 172.7 %all_gather.1 = bf16[4,2,2,2,29,18,8,128]{7,6,5,4,3,2,1,0:T(8,128)(2,1)} custom-call(bf16[30,18,8,128]{3,2,1,0:T(8,128)(2,1)} %to_tiles.1.a_ref), custom_call_target="tpu_custom_call" | custom-call | tf_op jit(solution)/shard_map/all_gather/pallas_call | solution.py:486
  552.0 22.9 %unpack.1 = (bf16[500,18,8,128]{3,2,1,0:T(8,128)(2,1)}, bf16[6,4,18,8,128]{4,3,2,1,0:T(8,128)(2,1)}, bf16[6,2,18,8,128]{4,3,2,1,0:T(8,128)(2,1)}, bf16[6,2,18,8,...) custom-call(bf16[32,29,18,8,128]{4,3,2,1,0:T(8,128)(2,1)} %bitcast.118), custom_call_target="tpu_custom_call" | custom-call | tf_op jit(solution)/shard_map/unpack/pallas_call | solution.py:161
  574.9 0.9 slice.38
  575.8 1.0 slice.39
  576.8 0.6 slice.43
  577.4 0.7 reshape.141
  (2 shorter events, 0.0 us)
Async XLA Ops:
  340.6 12.8 %copy-start.1 = (f32[517920]{0:T(1024)S(1)}, f32[517920]{0:T(1024)}, u32[]{:S(2)}) copy-start(f32[517920]{0:T(1024)} %param.26) | copy-start | bytes 6215044
  362.7 3.5 copy-start
  362.8 4.3 collective-permute-start
  367.1 0.7 copy-start.2

commit v2 on v1

--- a/solution.py
+++ b/solution.py
@@ -75,56 +75,16 @@
                 layer, col = divmod(first + k, TILES)
                 pairs.append((ref.at[layer, :, col], slot_ref.at[slot + k]))
         else:
-            step = 2 if kind == Q else 1
-            for k in range(0, count, step):
-                layer, half = divmod((first + k) // step, 2)
-                for row in range(2 * step):
-                    part = slot_ref.at[slot + k + row // 2, pl.ds(HALF * (row % 2), HALF)]
-                    pairs.append((ref.at[layer, row, pl.ds(HALF * half, HALF)], part))
+            per = 2 if kind == Q else 1
+            for k in range(count):
+                pair, odd = divmod(first + k, per)
+                layer, half = divmod(pair, 2)
+                for row in range(2):
+                    part = slot_ref.at[slot + k, pl.ds(HALF * row, HALF)]
+                    pairs.append((ref.at[layer, 2 * odd + row, pl.ds(HALF * half, HALF)], part))
     return pairs
 
 SLOTS = 8
-
-
-def pack_kernel(*args):
-    refs, (out_ref, stage, in_sem, out_sem) = args[:TENSORS], args[TENSORS:]
-    depth = stage.shape[0]
-
-    def start_in(r):
-        slot = r % depth
-        if r >= depth:
-            pltpu.make_async_copy(stage.at[slot], out_ref.at[r - depth], out_sem.at[slot]).wait()
-        for src, dst in tile_copies(refs, unit_runs(COVER_FIRST[r], COVER_FIRST[r] + COVER), stage.at[slot]):
-            pltpu.make_async_copy(src, dst, in_sem.at[slot]).start()
-
-    ahead = depth // 2
-    for r in range(ahead):
-        start_in(r)
-    for r in range(DEVICES):
-        if r + ahead < DEVICES:
-            start_in(r + ahead)
-        slot = r % depth
-        pltpu.make_async_copy(out_ref.at[r], stage.at[slot], in_sem.at[slot]).wait()
-        pltpu.make_async_copy(stage.at[slot], out_ref.at[r], out_sem.at[slot]).start()
-    for r in range(DEVICES - depth, DEVICES):
-        slot = r % depth
-        pltpu.make_async_copy(stage.at[slot], out_ref.at[r], out_sem.at[slot]).wait()
-
-
-def pack(tensors):
-    return pl.pallas_call(
-        pack_kernel,
-        name="pack",
-        out_shape=jax.ShapeDtypeStruct((DEVICES, COVER) + TAIL, jnp.bfloat16),
-        in_specs=[ANY] * TENSORS,
-        out_specs=ANY,
-        scratch_shapes=[
-            pltpu.VMEM((SLOTS, COVER) + TAIL, jnp.bfloat16),
-            pltpu.SemaphoreType.DMA((SLOTS,)),
-            pltpu.SemaphoreType.DMA((SLOTS,)),
-        ],
-        compiler_params=pltpu.CompilerParams(vmem_limit_bytes=BIG_VMEM),
-    )(*tensors)
 
 
 def unpack_kernel(*args):
@@ -204,27 +164,35 @@
 
 
 COLORS = range(4)
-OUTER = 7
-
-
-def jobs_of(sizes, first=0):
-    steps = [[] for _ in sizes[0]]
-    for color in COLORS:
-        for step, count in enumerate(sizes[color]):
-            if count:
-                steps[step].append((color, first, count))
-                first += count
+OUTER = 8
+DEPTH = 3
+
+
+def jobs_of(plan):
+    steps, first = [], 0
+    for colors in plan:
+        steps.append([(color, first + k, k) for k, color in enumerate(colors)])
+        first += len(colors)
     return steps
 
 
-RS_WIDE, RS_THIN = (1,) * 10, (1, 0) * 5
-RS_STEPS = jobs_of((RS_WIDE, RS_WIDE, RS_THIN, RS_THIN))
+RS_STEPS = jobs_of(((0, 1, 2), (0, 3, 2), (1, 2, 3), (0, 1, 3)) * 2 + ((0, 1, 2), (0, 1, 3)))
+
+
+class Line:
+    def __init__(self):
+        z, y, x, c = place()
+        self.inner = (z == 1) | (z == 2)
+        self.end = jnp.logical_not(self.inner)
+        self.near = z + 1 - 2 * (z % 2)
+        self.cross = (z + 2) % LINE
+        self.far = LINE - 1 - z
+        self.peers = [index_of(zz, y, x, c) for zz in (self.near, self.cross, self.far)]
 
 
 class Reduce:
-    def __init__(self, job, x_ref, g_ref, own, sum1, own_sem, sum_slot, got1, got2, got3, send, recv):
-        self.color, self.first, self.count = job
-        self.units = pl.ds(self.first, self.count)
+    def __init__(self, job, slot, g_ref, stage, sum1, got1, got2, got3, send, recv):
+        self.color, self.unit, k = job
         self.g_ref = g_ref
         z, y, x, c = place()
         self.z = z
@@ -234,69 +202,137 @@
         if by_x:
             group = ((y, 1 - x, c), (y, 1 - x, 1 - c), (y, x, 1 - c))
             side = index_of(z, 1 - y, x, c)
-            part = lambda yy, xx, cc: x_ref.at[:, :, xx, cc, self.units]
+            part = lambda yy, xx, cc: stage.at[slot, :, :, xx, cc, k]
         else:
             group = ((1 - y, x, c), (1 - y, x, 1 - c), (y, x, 1 - c))
             side = index_of(z, y, 1 - x, c)
-            part = lambda yy, xx, cc: x_ref.at[:, yy, :, cc, self.units]
-        n = pl.ds(0, self.count)
-        self.own = own.at[sum_slot, self.color, :, :, n]
-        self.sum1 = sum1.at[sum_slot, self.color, :, :, n]
+            part = lambda yy, xx, cc: stage.at[slot, :, yy, :, cc, k]
+        self.own = part(y, x, c)
+        self.sum1 = sum1.at[k]
         self.got1, self.got2, self.got3 = got1, got2, got3
         sems = Sems(send, recv)
-        self.copies1 = [sems.copy(part(*who), got1.at[k], index_of(z, *who)) for k, who in enumerate(group)]
-        self.own_copy = pltpu.make_async_copy(part(y, x, c), self.own, own_sem.at[sum_slot, self.color])
-        others = [(z + k) % LINE for k in range(1, LINE)]
-        peers = [index_of(zz, y, x, c) for zz in others]
+        self.copies1 = [sems.copy(part(*who), got1.at[i], index_of(z, *who)) for i, who in enumerate(group)]
+        line = Line()
+        self.line = line
         if self.late:
-            self.copies2 = [sems.copy(self.sum1.at[zz], got2.at[k], peer) for k, (zz, peer) in enumerate(zip(others, peers))]
-            self.copies3 = [sems.copy(got2.at[0, 1 - self.mine], got3.at[0], side)]
+            self.side = sems.copy(got2.at[0, 1 - self.mine], got3.at[0], side)
+            self.from_z, self.to_z = got2, lambda zz: self.sum1.at[zz]
         else:
-            self.copies2 = [sems.copy(self.sum1.at[:, 1 - self.mine], got2, side)]
-            self.copies3 = [sems.copy(got2.at[zz], got3.at[k], peer) for k, (zz, peer) in enumerate(zip(others, peers))]
-
-    def add1(self):
+            self.side = sems.copy(self.sum1.at[:, 1 - self.mine], got2, side)
+            self.from_z, self.to_z = got3, lambda zz: got2.at[zz]
+        near, cross, far = line.peers
+        self.near = sems.copy(self.to_z(line.near), self.from_z.at[0], near)
+        self.cross = sems.copy(self.to_z(line.cross), self.from_z.at[1], cross)
+        self.direct = sems.copy(self.to_z(line.far), self.from_z.at[2], far)
+        self.relay = sems.copy(self.to_z(line.far), self.from_z.at[3], near)
+
+    def start_line(self):
+        self.near.start()
+
+        @pl.when(self.line.inner)
+        def _():
+            self.direct.start()
+
+        @pl.when(self.line.end)
+        def _():
+            self.relay.start()
+            self.cross.start()
+
+    def pass_on(self):
+        @pl.when(self.line.inner)
+        def _():
+            self.relay.wait_recv()
+            held, more = self.to_z(self.line.cross), self.from_z.at[3]
+            if self.late:
+                for side in range(2):
+                    held[side] = held[side] + more[side]
+            else:
+                held[...] = held[...] + more[...]
+            self.cross.start()
+
+    def recv_line(self):
+        self.near.wait_recv()
+        self.cross.wait_recv()
+
+        @pl.when(self.line.inner)
+        def _():
+            self.direct.wait_recv()
+
+    def line_total(self, pick):
+        total = pick(self.to_z(self.z)) + pick(self.from_z.at[0]) + pick(self.from_z.at[1])
+        return total + jnp.where(self.line.inner, pick(self.from_z.at[2]), 0.0)
+
+    def sent_line(self):
+        self.near.wait_send()
+        self.cross.wait_send()
+
+        @pl.when(self.line.inner)
+        def _():
+            self.direct.wait_send()
+
+        @pl.when(self.line.end)
+        def _():
+            self.relay.wait_send()
+
+    def sent_sums(self):
+        if self.late:
+            self.sent_line()
+        else:
+            self.side.wait_send()
+
+    def sent_rest(self):
+        if self.late:
+            self.side.wait_send()
+        else:
+            self.sent_line()
+
+    def phase0(self):
+        recv_all(self.copies1)
+
         def body(i, carry):
-            zz, side, u = i // (2 * self.count), (i // self.count) % 2, i % self.count
-            total = self.own[zz, side, u].astype(jnp.float32)
+            zz, side = i // 2, i % 2
+            total = self.own[zz, side].astype(jnp.float32)
             for k in range(len(self.copies1)):
-                total = total + self.got1[k, zz, side, u].astype(jnp.float32)
-            self.sum1[zz, side, u] = total
+                total = total + self.got1[k, zz, side].astype(jnp.float32)
+            self.sum1[zz, side] = total
             return carry
 
-        lax.fori_loop(0, 2 * LINE * self.count, body, 0)
-
-    def add2(self):
-        def early(i, carry):
-            zz, u = i // self.count, i % self.count
-            self.got2[zz, u] = self.got2[zz, u] + self.sum1[zz, self.mine, u]
+        lax.fori_loop(0, 2 * LINE, body, 0)
+        return self.start_line if self.late else self.side.start
+
+    def phase1(self):
+        if self.late:
+            self.pass_on()
+            return None
+        self.side.wait_recv()
+
+        def body(zz, carry):
+            self.got2[zz] = self.got2[zz] + self.sum1[zz, self.mine]
             return carry
 
-        def late(i, carry):
-            side, u = i // self.count, i % self.count
-            total = self.sum1[self.z, side, u]
-            for k in range(LINE - 1):
-                total = total + self.got2[k, side, u]
-            self.got2[0, side, u] = total
-            return carry
-
+        lax.fori_loop(0, LINE, body, 0)
+        return self.start_line
+
+    def phase2(self):
+        if not self.late:
+            self.pass_on()
+            return None
+        self.recv_line()
+        for side in range(2):
+            self.got2[0, side] = self.line_total(lambda ref: ref[side])
+        return self.side.start
+
+    def phase3(self, begin, end, acc):
         if self.late:
-            lax.fori_loop(0, 2 * self.count, late, 0)
+            self.side.wait_recv()
+            total = self.got2[0, self.mine] + self.got3[0]
         else:
-            lax.fori_loop(0, LINE * self.count, early, 0)
-
-    def add3(self, begin, end, acc):
-        def body(u, acc):
-            total = self.got2[0, self.mine, u] if self.late else self.got2[self.z, u]
-            for k in range(len(self.copies3)):
-                total = total + self.got3[k, u]
-            mean = total * (1.0 / DEVICES)
-            slot = self.first + u
-            self.g_ref[slot] = mean
-            square = jnp.sum(mean * mean, axis=0)
-            return acc + jnp.where((slot >= begin) & (slot < end), square, 0.0)
-
-        return lax.fori_loop(0, self.count, body, acc)
+            self.recv_line()
+            total = self.line_total(lambda ref: ref[...])
+        mean = total * (1.0 / DEVICES)
+        self.g_ref[self.unit] = mean
+        square = jnp.sum(mean * mean, axis=0)
+        return acc + jnp.where((self.unit >= begin) & (self.unit < end), square, 0.0)
 
 
 def start_all(copies):
@@ -315,55 +351,64 @@
 
 
 def reduce_kernel(*args):
-    x_ref, g_ref, n_ref, own, sum1, norm_buf, own_sem, send_n, recv_n = args[:9]
-    rest = list(args[9:])
+    tensors, (g_ref, n_ref, stage, sum1, norm_buf, in_sem, send_n, recv_n) = args[:TENSORS], args[TENSORS:TENSORS + 8]
+    rest = args[TENSORS + 8:]
     z, y, x, c = place()
     me = lax.axis_index("dp")
-    z_peers = [index_of((z + k) % LINE, y, x, c) for k in range(1, LINE)]
-    plane = [index_of(z, y, x, 1 - c), index_of(z, y, 1 - x, c), index_of(z, y, 1 - x, 1 - c), index_of(z, 1 - y, x, c), index_of(z, 1 - y, x, 1 - c)]
-    greet(plane + z_peers)
     steps = []
     for t, jobs in enumerate(RS_STEPS):
         steps.append([])
         for job in jobs:
-            steps[t].append(Reduce(job, x_ref, g_ref, own, sum1, own_sem, t % 2, *rest[:5]))
+            steps[t].append(Reduce(job, t % DEPTH, g_ref, stage, sum1.at[t % DEPTH], *rest[:5]))
             rest = rest[5:]
-    total_steps = len(steps)
+    count = len(steps)
+
+    def start_in(t):
+        if t < count:
+            slot, first, units = t % DEPTH, steps[t][0].unit, len(steps[t])
+            for r in range(DEVICES):
+                zyx, core = divmod(r, 2)
+                zy, xx = divmod(zyx, 2)
+                zz, yy = divmod(zy, 2)
+                runs = unit_runs(COVER_FIRST[r] + first, COVER_FIRST[r] + first + units)
+                for src, dst in tile_copies(tensors, runs, stage.at[slot, zz, yy, xx, core]):
+                    pltpu.make_async_copy(src, dst, in_sem.at[slot]).start()
 
     def start1(t):
-        for k in range(3):
-            for job in steps[t]:
-                job.copies1[k].start()
-        for job in steps[t]:
-            job.own_copy.start()
-
+        if t < count:
+            part = stage.at[t % DEPTH, :, :, :, :, pl.ds(0, len(steps[t]))]
+            pltpu.make_async_copy(part, part, in_sem.at[t % DEPTH]).wait()
+            for k in range(3):
+                for job in steps[t]:
+                    job.copies1[k].start()
+
+    for t in range(DEPTH):
+        start_in(t)
+    z_peers = Line().peers
+    plane = [index_of(z, y, x, 1 - c), index_of(z, y, 1 - x, c), index_of(z, y, 1 - x, 1 - c), index_of(z, 1 - y, x, c), index_of(z, 1 - y, x, 1 - c)]
+    greet(plane + z_peers)
     first = first_unit(me)
     begin = first - jnp.minimum(first, END - COVER)
     end = begin + first_unit(me + 1) - first
     acc = jnp.zeros((SUB, LANES), jnp.float32)
     start1(0)
-    for t in range(total_steps + 2):
-        if t + 1 < total_steps:
-            start1(t + 1)
-        if t < total_steps:
+    for t in range(count + 3):
+        start1(t + 1)
+        if t < count:
+            if t >= DEPTH:
+                for job in steps[t - DEPTH]:
+                    job.sent_sums()
+            start_all([Later(job.phase0()) for job in steps[t]])
             for job in steps[t]:
-                recv_all(job.copies1)
-                job.own_copy.wait()
-                if t >= 2:
-                    send_all([copy for old in steps[t - 2] if old.color == job.color for copy in old.copies2])
-                job.add1()
-            for job in steps[t]:
-                start_all(job.copies2)
-        if 1 <= t <= total_steps:
-            for job in steps[t - 1]:
-                recv_all(job.copies2)
-                job.add2()
-            for job in steps[t - 1]:
-                start_all(job.copies3)
-        if t >= 2:
-            for job in steps[t - 2]:
-                recv_all(job.copies3)
-                acc = job.add3(begin, end, acc)
+                send_all(job.copies1)
+            start_in(t + DEPTH)
+        if 1 <= t <= count:
+            start_all([Later(job.phase1()) for job in steps[t - 1]])
+        if 2 <= t <= count + 1:
+            start_all([Later(job.phase2()) for job in steps[t - 2]])
+        if t >= 3:
+            for job in steps[t - 3]:
+                acc = job.phase3(begin, end, acc)
 
     sems = Sems(send_n, recv_n)
     sent, used = [], 0
@@ -383,21 +428,30 @@
     send_all(sent)
     for t, jobs in enumerate(steps):
         for job in jobs:
-            send_all(job.copies1 + job.copies3)
-            if not any(later.color == job.color for later in sum(steps[t + 2:t + 3], [])):
-                send_all(job.copies2)
-
-
-def reduce_scatter(packed):
+            if t >= count - DEPTH:
+                job.sent_sums()
+            job.sent_rest()
+
+
+class Later:
+    def __init__(self, action):
+        self.action = action
+
+    def start(self):
+        if self.action is not None:
+            self.action()
+
+
+def reduce_scatter(tensors):
     dma = pltpu.SemaphoreType.DMA
     scratch = []
-    largest = max(RS_WIDE)
-    for color, first, count in sum(RS_STEPS, []):
+    most = max(len(jobs) for jobs in RS_STEPS)
+    for color, unit, k in sum(RS_STEPS, []):
         late = color >= 2
         scratch += [
-            pltpu.VMEM((3, LINE, 2, count) + TAIL, jnp.bfloat16),
-            pltpu.VMEM(((3, 2, count) if late else (LINE, count)) + TAIL, jnp.float32),
-            pltpu.VMEM((1 if late else 3, count) + TAIL, jnp.float32),
+            pltpu.VMEM((3, LINE, 2) + TAIL, jnp.bfloat16),
+            pltpu.VMEM(((LINE, 2) if late else (LINE,)) + TAIL, jnp.float32),
+            pltpu.VMEM((1 if late else LINE,) + TAIL, jnp.float32),
             dma((OUTER,)),
             dma((OUTER,)),
         ]
@@ -405,80 +459,119 @@
         reduce_kernel,
         name="reduce_scatter",
         out_shape=[jax.ShapeDtypeStruct((COVER,) + TAIL, jnp.float32), jax.ShapeDtypeStruct((1,), jnp.float32)],
-        in_specs=[ANY],
+        in_specs=[ANY] * TENSORS,
         out_specs=[IN_VMEM, IN_SMEM],
         scratch_shapes=[
-            pltpu.VMEM((2, len(COLORS), LINE, 2, largest) + TAIL, jnp.bfloat16),
-            pltpu.VMEM((2, len(COLORS), LINE, 2, largest) + TAIL, jnp.float32),
+            pltpu.VMEM((DEPTH, LINE, 2, 2, 2, most) + TAIL, jnp.bfloat16),
+            pltpu.VMEM((DEPTH, most, LINE, 2) + TAIL, jnp.float32),
             pltpu.VMEM((11, SUB, LANES), jnp.float32),
-            dma((2, len(COLORS))),
+            dma((DEPTH,)),
             dma((OUTER,)),
             dma((OUTER,)),
         ] + scratch,
         compiler_params=pltpu.CompilerParams(collective_id=0, has_side_effects=True, vmem_limit_bytes=BIG_VMEM),
-    )(packed.reshape((LINE, 2, 2, 2, COVER) + TAIL))
-
-
-AG_STEPS = jobs_of(((1,) * 10, (1,) * 9 + (0,), (1, 0) * 5, (1, 0) * 5))
+    )(*tensors)
+
+
+AG_STEPS = jobs_of(((0, 1, 2), (0, 1, 3)) * 4 + ((0, 1, 2), (0, 3)))
 
 
 class Gather:
     def __init__(self, job, a_ref, b_ref, send, recv):
-        color, first, count = job
-        u = pl.ds(first, count)
+        color, unit, _ = job
+        u = pl.ds(unit, 1)
         z, y, x, c = place()
-        z_peers = [index_of((z + k) % LINE, y, x, c) for k in range(1, LINE)]
         y_peer, x_peer, c_peer = index_of(z, 1 - y, x, c), index_of(z, y, 1 - x, c), index_of(z, y, x, 1 - c)
         by_x = color % 2 == 0
         side, last = (y_peer, x_peer) if by_x else (x_peer, y_peer)
         sems = Sems(send, recv)
         here, row = b_ref.at[z, y, x, c, u], b_ref.at[:, y, x, c, u]
-        pair = b_ref.at[z, :, x, c, u] if by_x else b_ref.at[z, y, :, c, u]
         half = b_ref.at[:, :, x, c, u] if by_x else b_ref.at[:, y, :, c, u]
         full = b_ref.at[:, :, :, c, u]
-        if color < 2:
-            self.stages = [[sems.copy(a_ref.at[u], here, peer) for peer in z_peers], [sems.copy(row, row, side)]]
+        self.late = color >= 2
+        if self.late:
+            at = lambda zz: b_ref.at[zz, :, x, c, u] if by_x else b_ref.at[zz, y, :, c, u]
+            source, self.side = at(z), sems.copy(a_ref.at[u], here, side)
         else:
-            self.stages = [[sems.copy(a_ref.at[u], here, side)], [sems.copy(pair, pair, peer) for peer in z_peers]]
-        self.stages += [[sems.copy(half, half, last)], [sems.copy(full, full, c_peer)]]
+            at = lambda zz: b_ref.at[zz, y, x, c, u]
+            source, self.side = a_ref.at[u], sems.copy(row, row, side)
+        self.line = line = Line()
+        self.near, self.cross, self.direct = (sems.copy(source, at(z), peer) for peer in line.peers)
+        self.relay = sems.copy(at(line.cross), at(line.cross), line.peers[0])
+        self.half, self.full = sems.copy(half, half, last), sems.copy(full, full, c_peer)
+
+    def start_line(self):
+        self.near.start()
+        self.cross.start()
+
+        @pl.when(self.line.inner)
+        def _():
+            self.direct.start()
+
+    def pass_on(self):
+        @pl.when(self.line.inner)
+        def _():
+            self.cross.wait_recv()
+            self.relay.start()
+
+    def recv_line(self):
+        self.near.wait_recv()
+
+        @pl.when(self.line.inner)
+        def _():
+            self.direct.wait_recv()
+
+        @pl.when(self.line.end)
+        def _():
+            self.cross.wait_recv()
+            self.relay.wait_recv()
+
+    def phases(self):
+        nothing = lambda: None
+        if self.late:
+            first = [(nothing, self.side.start), (self.side.wait_recv, self.start_line), (nothing, self.pass_on), (self.recv_line, self.half.start)]
+        else:
+            first = [(nothing, self.start_line), (nothing, self.pass_on), (self.recv_line, self.side.start), (self.side.wait_recv, self.half.start)]
+        return first + [(self.half.wait_recv, self.full.start), (self.full.wait_recv, nothing)]
+
+    def sent(self):
+        for copy in (self.side, self.near, self.cross, self.half, self.full):
+            copy.wait_send()
+
+        @pl.when(self.line.inner)
+        def _():
+            self.direct.wait_send()
+            self.relay.wait_send()
 
 
 def gather_kernel(a_ref, b_ref, own_sem, *rest):
     z, y, x, c = place()
-    z_peers = [index_of((z + k) % LINE, y, x, c) for k in range(1, LINE)]
-    greet(z_peers + [index_of(z, 1 - y, x, c), index_of(z, y, 1 - x, c), index_of(z, y, x, 1 - c)])
+    greet(Line().peers + [index_of(z, 1 - y, x, c), index_of(z, y, 1 - x, c), index_of(z, y, x, 1 - c)])
     own = pltpu.make_async_copy(a_ref.at[pl.ds(0, GATHER)], b_ref.at[z, y, x, c], own_sem)
     own.start()
-    steps = []
+    steps, made = [], []
     for jobs in AG_STEPS:
         steps.append([])
         for job in jobs:
-            steps[-1].append(Gather(job, a_ref, b_ref, *rest[:2]))
+            made.append(Gather(job, a_ref, b_ref, *rest[:2]))
+            steps[-1].append(made[-1].phases())
             rest = rest[2:]
-    count, stages = len(steps), 4
-
-    def start(t, stage):
+    count, phases = len(steps), len(steps[0][0])
+
+    def run(t, phase):
         if 0 <= t < count:
-            if stage:
-                for job in steps[t]:
-                    recv_all(job.stages[stage - 1])
-                    start_all(job.stages[stage])
-            else:
-                for job in steps[t]:
-                    start_all(job.stages[0])
-
-    start(0, 0)
-    start(1, 0)
+            for job in steps[t]:
+                job[phase][0]()
+                job[phase][1]()
+
+    run(0, 0)
     own.wait()
-    for t in range(count + stages):
-        start(t + 2, 0)
-        for stage in range(1, stages):
-            start(t + 1 - stage, stage)
-    for jobs in steps:
-        for job in jobs:
-            recv_all(job.stages[-1])
-            for copies in job.stages:
-                send_all(copies)
+    for t in range(count + phases):
+        run(t + 1, 0)
+        for phase in range(1, phases):
+            run(t + 1 - phase, phase)
+    for job in made:
+        job.sent()
 
 
 def all_gather(chunk):
@@ -754,7 +847,7 @@
         blank = jnp.zeros(((END - NORMS) * UNIT - NORM_LEN,), jnp.bfloat16)
         small = jnp.concatenate([arr.reshape(-1) for arr in grads[TENSORS - 1:]] + [blank])
         tensors.append(small.reshape((END - NORMS,) + TAIL))
-        grad_tiles, squares = reduce_scatter(pack(tensors))
+        grad_tiles, squares = reduce_scatter(tensors)
         clip_scale = jnp.minimum(1.0, hyper_params[4] / (jnp.sqrt(squares[0]) + CLIP_EPS))
         grad_part = to_flat(grad_tiles).reshape(-1)[:SHARD]
         keep_decay = me * SHARD + lax.broadcasted_iota(jnp.int32, (SHARD,), 0) < SHARD * DEVICES - NORM_LEN

time: 579 us -> 523 us (0.903)
  the two profiles are of different devices: /device:TPU:27 before, /device:TPU:3 now
where the time goes in v2:
time: 523 us; the launch traced here: 521 us
  Pallas kernels  491 us (94%)
  other arithmetic  9.94 us (2%)
  local copies, waits for them, and re-layouts  8.49 us (2%)
  between operations  7.2 us (1%)
    pallas_call x1, Pallas kernels, reduce_scatter(): pl.pallas_call(reduce_kernel, name='reduce_scatter', out_shape=[jax.Shape...  293 us
    pallas_call x1, Pallas kernels, all_gather(): pl.pallas_call(gather_kernel, name='all_gather', out_shape=jax.ShapeDtype...  162 us
    pallas_call x1, Pallas kernels, unpack(): pl.pallas_call(unpack_kernel, name='unpack', out_shape=[jax.ShapeDtypeStr...  22.9 us
  transfers between devices with their start and end apart: 1, of which 1 were waited for; matrix products, arithmetic and copies ran while one was open for 0% of the time, Pallas kernels for 0%

profile of v2, /device:TPU:3, one launch (start us, length us, event | category | flops | bytes accessed | tf_op | source)
XLA Modules:
  0.0 521.2 jit_solution(3627858834312570665)
XLA Ops:
  0.6 1.4 fusion
  7.3 0.7 copy.27
  8.0 0.9 reshape.123
  8.9 0.7 pad_maximum_fusion
  9.6 292.8 %reduce_scatter.1 = (f32[30,18,8,128]{3,2,1,0:T(8,128)}, f32[1]{0:T(128)}) custom-call(bf16[500,18,8,128]{3,2,1,0:T(8,128)(2,1)} %bitcast.117, bf16[6,4,18,8,128]{4,3,2,1,0:T(8,128)(2,1)} %bitcast.123, bf16[6,2,18,8,128]{4,3,2,1,0:T(8,128)(2,1)} %bitcast.126, bf16[6,2,18,8,128]{4,3,2,1,0:T(8,128)(2,1)} %bitcast.127, bf16[24,18,8,128]{3,2,1,0:T(8,128)(2,1)} %bitcast.124, ...), custom_call_target="tpu_custom_call" | custom-call | tf_op jit(solution)/shard_map/reduce_scatter/pallas_call | solution.py:458
  303.0 0.0 copy-start.1
  303.1 6.7 %to_flat.1 = f32[4048,128]{1,0:T(8,128)} custom-call(f32[4320,128]{1,0:T(8,128)} %bitcast.122), custom_call_target="tpu_custom_call" | custom-call | tf_op jit(solution)/shard_map/to_flat/pallas_call | solution.py:754
  310.4 0.0 copy-done.1
  310.5 9.3 %multiply_subtract_fusion = (f32[517920]{0:T(1024)S(1)}, f32[517920]{0:T(1024)}, f32[517920]{0:T(1024)}) fusion(f32[517920]{0:T(1024)S(1)} %copy-done.1, f32[]{:T(128)} %bitcast.38, s32[]{:T(128)S(6)} %mul.92, f32[]{:T(128)S(6)} %sub.18, f32[]{:T(128)S(6)} %sub.16, f32[]{:T(128)} %bitcast, f32[]{:T(128)} %bitcast.36, f32[518144]{0:T(1024)} %bitcast.118, ...), kind=kLoop, calls=%fused_computation.2 | loop fusion | flops 9840480 | bytes 14501800 | tf_op jit(solution)/shard_map/sub | solution.py:821
  319.7 0.0 copy-start
  319.7 0.1 slice.42
  319.8 4.4 collective-permute-start
  324.3 1.4 pad_bitcast_fusion.in_ref
  325.7 0.0 copy-done
  325.7 0.5 collective-permute-done
  326.2 0.0 copy-start.2
  326.2 0.7 copy-done.2
  326.8 6.5 %to_tiles.1.a_ref = bf16[30,18,8,128]{3,2,1,0:T(8,128)(2,1)} custom-call(f32[288,128]{1,0:T(8,128)} %bitcast.128, f32[4048,128]{1,0:T(8,128)} %pad_bitcast_fusion.in_ref), custom_call_target="tpu_custom_call" | custom-call | tf_op jit(solution)/shard_map/to_tiles/pallas_call | solution.py:803
  333.3 161.8 %all_gather.1 = bf16[4,2,2,2,29,18,8,128]{7,6,5,4,3,2,1,0:T(8,128)(2,1)} custom-call(bf16[30,18,8,128]{3,2,1,0:T(8,128)(2,1)} %to_tiles.1.a_ref), custom_call_target="tpu_custom_call" | custom-call | tf_op jit(solution)/shard_map/all_gather/pallas_call | solution.py:579
  495.2 22.9 %unpack.1 = (bf16[500,18,8,128]{3,2,1,0:T(8,128)(2,1)}, bf16[6,4,18,8,128]{4,3,2,1,0:T(8,128)(2,1)}, bf16[6,2,18,8,128]{4,3,2,1,0:T(8,128)(2,1)}, bf16[6,2,18,8,...) custom-call(bf16[32,29,18,8,128]{4,3,2,1,0:T(8,128)(2,1)} %bitcast.116), custom_call_target="tpu_custom_call" | custom-call | tf_op jit(solution)/shard_map/unpack/pallas_call | solution.py:121
  518.0 0.9 slice.38
  518.9 1.0 slice.39
  520.0 0.6 slice.43
  520.6 0.7 reshape.137
  (1 shorter events, 0.0 us)
Async XLA Ops:
  303.0 7.4 %copy-start.1 = (f32[517920]{0:T(1024)S(1)}, f32[517920]{0:T(1024)}, u32[]{:S(2)}) copy-start(f32[517920]{0:T(1024)} %param.26) | copy-start | bytes 6215044
  319.7 6.0 %copy-start = (f32[517920]{0:T(1024)}, f32[517920]{0:T(1024)S(1)}, u32[]{:S(2)}) copy-start(f32[517920]{0:T(1024)S(1)} %get-tuple-element.35) | copy-start | bytes 6215044
  319.8 6.3 %collective-permute-start = (f32[36864]{0:T(1024)S(1)}, f32[36864]{0:T(1024)S(1)}, u32[]{:S(2)}, u32[]{:S(2)}) collective-permute-start(f32[36864]{0:T(1024)S(1)} %slice.42), channel_id=1, source_target_pairs={{0,1},{1,2},{2,3},{3,4},{4,5},{5,6},{6,7},{7,8},{8,9},{9,10},{10,1... | collective-permute-start | bytes 442376 | tf_op jit(solution)/shard_map/ppermute | solution.py:855
  326.2 0.7 copy-start.2

commit v3 on v2

--- a/solution.py
+++ b/solution.py
@@ -166,6 +166,8 @@
 COLORS = range(4)
 OUTER = 8
 DEPTH = 3
+AHEAD = 1
+PHASE = (0, 1, 3, 5)
 
 
 def jobs_of(plan):
@@ -176,7 +178,7 @@
     return steps
 
 
-RS_STEPS = jobs_of(((0, 1, 2), (0, 3, 2), (1, 2, 3), (0, 1, 3)) * 2 + ((0, 1, 2), (0, 1, 3)))
+RS_STEPS = jobs_of(((0, 3), (2, 1), (2, 3)) * 5)
 
 
 class Line:
@@ -355,11 +357,11 @@
     rest = args[TENSORS + 8:]
     z, y, x, c = place()
     me = lax.axis_index("dp")
-    steps = []
+    steps, sums = [], PHASE[2] + 1
     for t, jobs in enumerate(RS_STEPS):
         steps.append([])
         for job in jobs:
-            steps[t].append(Reduce(job, t % DEPTH, g_ref, stage, sum1.at[t % DEPTH], *rest[:5]))
+            steps[t].append(Reduce(job, t % DEPTH, g_ref, stage, sum1.at[t % sums], *rest[:5]))
             rest = rest[5:]
     count = len(steps)
 
@@ -391,23 +393,24 @@
     begin = first - jnp.minimum(first, END - COVER)
     end = begin + first_unit(me + 1) - first
     acc = jnp.zeros((SUB, LANES), jnp.float32)
-    start1(0)
-    for t in range(count + 3):
-        start1(t + 1)
+    for t in range(AHEAD):
+        start1(t)
+    for t in range(count + PHASE[3]):
+        start1(t + AHEAD)
         if t < count:
-            if t >= DEPTH:
-                for job in steps[t - DEPTH]:
+            if t >= sums:
+                for job in steps[t - sums]:
                     job.sent_sums()
             start_all([Later(job.phase0()) for job in steps[t]])
             for job in steps[t]:
                 send_all(job.copies1)
             start_in(t + DEPTH)
-        if 1 <= t <= count:
-            start_all([Later(job.phase1()) for job in steps[t - 1]])
-        if 2 <= t <= count + 1:
-            start_all([Later(job.phase2()) for job in steps[t - 2]])
-        if t >= 3:
-            for job in steps[t - 3]:
+        if 0 <= t - PHASE[1] < count:
+            start_all([Later(job.phase1()) for job in steps[t - PHASE[1]]])
+        if 0 <= t - PHASE[2] < count:
+            start_all([Later(job.phase2()) for job in steps[t - PHASE[2]]])
+        if 0 <= t - PHASE[3]:
+            for job in steps[t - PHASE[3]]:
                 acc = job.phase3(begin, end, acc)
 
     sems = Sems(send_n, recv_n)
@@ -428,7 +431,7 @@
     send_all(sent)
     for t, jobs in enumerate(steps):
         for job in jobs:
-            if t >= count - DEPTH:
+            if t >= count - sums:
                 job.sent_sums()
             job.sent_rest()
 
@@ -463,7 +466,7 @@
         out_specs=[IN_VMEM, IN_SMEM],
         scratch_shapes=[
             pltpu.VMEM((DEPTH, LINE, 2, 2, 2, most) + TAIL, jnp.bfloat16),
-            pltpu.VMEM((DEPTH, most, LINE, 2) + TAIL, jnp.float32),
+            pltpu.VMEM((PHASE[2] + 1, most, LINE, 2) + TAIL, jnp.float32),
             pltpu.VMEM((11, SUB, LANES), jnp.float32),
             dma((DEPTH,)),
             dma((OUTER,)),
@@ -473,7 +476,7 @@
     )(*tensors)
 
 
-AG_STEPS = jobs_of(((0, 1, 2), (0, 1, 3)) * 4 + ((0, 1, 2), (0, 3)))
+AG_STEPS = jobs_of(((0, 3), (2, 1), (2, 3)) * 4 + ((0, 3), (2, 1), (2,)))
 
 
 class Gather:

time: 523 us -> 501 us (0.958)
  Pallas kernels: 491 us -> 469 us
    pallas_call x1, Pallas kernels: 162 us -> 151 us  [all_gather(): pl.pallas_call(gather_kernel, name='all_gather', out_shape=jax.ShapeDtype...]
    pallas_call x1, Pallas kernels: 293 us -> 282 us  [reduce_scatter(): pl.pallas_call(reduce_kernel, name='reduce_scatter', out_shape=[jax.Shape...]
where the time goes in v3:
time: 501 us; the launch traced here: 500 us
  Pallas kernels  469 us (94%)
  other arithmetic  9.94 us (2%)
  local copies, waits for them, and re-layouts  8.49 us (2%)
  between operations  7.2 us (1%)
  starting transfers between devices  5.17 us (1%)
    pallas_call x1, Pallas kernels, reduce_scatter(): pl.pallas_call(reduce_kernel, name='reduce_scatter', out_shape=[jax.Shape...  282 us
    pallas_call x1, Pallas kernels, all_gather(): pl.pallas_call(gather_kernel, name='all_gather', out_shape=jax.ShapeDtype...  151 us
    pallas_call x1, Pallas kernels, unpack(): pl.pallas_call(unpack_kernel, name='unpack', out_shape=[jax.ShapeDtypeStr...  22.9 us
  transfers between devices with their start and end apart: 1, of which 1 were waited for; matrix products, arithmetic and copies ran while one was open for 0% of the time, Pallas kernels for 0%

profile of v3, /device:TPU:3, one launch (start us, length us, event | category | flops | bytes accessed | tf_op | source)
XLA Modules:
  0.0 500.3 jit_solution(11225897646044347366)
XLA Ops:
  0.6 1.4 fusion
  7.3 0.7 copy.27
  8.0 0.9 reshape.123
  8.9 0.7 pad_maximum_fusion
  9.6 282.2 %reduce_scatter.1 = (f32[30,18,8,128]{3,2,1,0:T(8,128)}, f32[1]{0:T(128)}) custom-call(bf16[500,18,8,128]{3,2,1,0:T(8,128)(2,1)} %bitcast.117, bf16[6,4,18,8,128]{4,3,2,1,0:T(8,128)(2,1)} %bitcast.123, bf16[6,2,18,8,128]{4,3,2,1,0:T(8,128)(2,1)} %bitcast.126, bf16[6,2,18,8,128]{4,3,2,1,0:T(8,128)(2,1)} %bitcast.127, bf16[24,18,8,128]{3,2,1,0:T(8,128)(2,1)} %bitcast.124, ...), custom_call_target="tpu_custom_call" | custom-call | tf_op jit(solution)/shard_map/reduce_scatter/pallas_call | solution.py:461
  292.5 0.0 copy-start.1
  292.5 6.7 %to_flat.1 = f32[4048,128]{1,0:T(8,128)} custom-call(f32[4320,128]{1,0:T(8,128)} %bitcast.122), custom_call_target="tpu_custom_call" | custom-call | tf_op jit(solution)/shard_map/to_flat/pallas_call | solution.py:757
  299.9 0.0 copy-done.1
  299.9 9.3 %multiply_subtract_fusion = (f32[517920]{0:T(1024)S(1)}, f32[517920]{0:T(1024)}, f32[517920]{0:T(1024)}) fusion(f32[517920]{0:T(1024)S(1)} %copy-done.1, f32[]{:T(128)} %bitcast.38, s32[]{:T(128)S(6)} %mul.92, f32[]{:T(128)S(6)} %sub.18, f32[]{:T(128)S(6)} %sub.16, f32[]{:T(128)} %bitcast, f32[]{:T(128)} %bitcast.36, f32[518144]{0:T(1024)} %bitcast.118, ...), kind=kLoop, calls=%fused_computation.2 | loop fusion | flops 9840480 | bytes 14501800 | tf_op jit(solution)/shard_map/sub | solution.py:824
  309.1 0.0 copy-start
  309.2 0.1 slice.42
  309.3 5.2 %collective-permute-start = (f32[36864]{0:T(1024)S(1)}, f32[36864]{0:T(1024)S(1)}, u32[]{:S(2)}, u32[]{:S(2)}) collective-permute-start(f32[36864]{0:T(1024)S(1)} %slice.42), channel_id=1, source_target_pairs={{0,1},{1,2},{2,3},{3,4},{4,5},{5,6},{6,7},{7,8},{8,9},{9,10},{10,1... | collective-permute-start | bytes 442376 | tf_op jit(solution)/shard_map/ppermute | solution.py:858
  314.4 1.4 pad_bitcast_fusion.in_ref
  315.9 0.0 copy-done
  315.9 0.5 collective-permute-done
  316.3 0.0 copy-start.2
  316.3 0.7 copy-done.2
  317.0 6.5 %to_tiles.1.a_ref = bf16[30,18,8,128]{3,2,1,0:T(8,128)(2,1)} custom-call(f32[288,128]{1,0:T(8,128)} %bitcast.128, f32[4048,128]{1,0:T(8,128)} %pad_bitcast_fusion.in_ref), custom_call_target="tpu_custom_call" | custom-call | tf_op jit(solution)/shard_map/to_tiles/pallas_call | solution.py:806
  323.5 150.7 %all_gather.1 = bf16[4,2,2,2,29,18,8,128]{7,6,5,4,3,2,1,0:T(8,128)(2,1)} custom-call(bf16[30,18,8,128]{3,2,1,0:T(8,128)(2,1)} %to_tiles.1.a_ref), custom_call_target="tpu_custom_call" | custom-call | tf_op jit(solution)/shard_map/all_gather/pallas_call | solution.py:582
  474.2 22.9 %unpack.1 = (bf16[500,18,8,128]{3,2,1,0:T(8,128)(2,1)}, bf16[6,4,18,8,128]{4,3,2,1,0:T(8,128)(2,1)}, bf16[6,2,18,8,128]{4,3,2,1,0:T(8,128)(2,1)}, bf16[6,2,18,8,...) custom-call(bf16[32,29,18,8,128]{4,3,2,1,0:T(8,128)(2,1)} %bitcast.116), custom_call_target="tpu_custom_call" | custom-call | tf_op jit(solution)/shard_map/unpack/pallas_call | solution.py:121
  497.1 0.9 slice.38
  498.0 1.0 slice.39
  499.0 0.6 slice.43
  499.6 0.7 reshape.137
  (1 shorter events, 0.0 us)
Async XLA Ops:
  292.5 7.4 %copy-start.1 = (f32[517920]{0:T(1024)S(1)}, f32[517920]{0:T(1024)}, u32[]{:S(2)}) copy-start(f32[517920]{0:T(1024)} %param.26) | copy-start | bytes 6215044
  309.1 6.7 %copy-start = (f32[517920]{0:T(1024)}, f32[517920]{0:T(1024)S(1)}, u32[]{:S(2)}) copy-start(f32[517920]{0:T(1024)S(1)} %get-tuple-element.35) | copy-start | bytes 6215044
  309.3 7.1 %collective-permute-start = (f32[36864]{0:T(1024)S(1)}, f32[36864]{0:T(1024)S(1)}, u32[]{:S(2)}, u32[]{:S(2)}) collective-permute-start(f32[36864]{0:T(1024)S(1)} %slice.42), channel_id=1, source_target_pairs={{0,1},{1,2},{2,3},{3,4},{4,5},{5,6},{6,7},{7,8},{8,9},{9,10},{10,1... | collective-permute-start | bytes 442376 | tf_op jit(solution)/shard_map/ppermute | solution.py:858
  316.3 0.7 copy-start.2

commit v4 on v3

--- a/solution.py
+++ b/solution.py
@@ -178,7 +178,7 @@
     return steps
 
 
-RS_STEPS = jobs_of(((0, 3), (2, 1), (2, 3)) * 5)
+RS_STEPS = jobs_of(((2, 3), (0, 3), (2, 1)) * 5)
 
 
 class Line:
@@ -671,7 +671,7 @@
     @pl.when(among(u, GATE, UP))
     def _():
         wide[...] = turned([tile(in_ref, unit, t)[...] for t in range(LANES // SUB)])
-        tail[...] = turned([tile(in_ref, unit, t)[...] for t in range(LANES // SUB, TILES)])
+        tail[:, 0:EDGE] = jnp.concatenate([tile(in_ref, unit, t)[...] for t in range(LANES // SUB, TILES)], axis=0).T
         lane = lanes(EDGE)
         before = None
         for j in range(SUB):
@@ -705,7 +705,7 @@
             wide[pl.ds(j, EDGE, stride=SUB), :] = rolled(jnp.where(lane >= EDGE * j, here, after), -EDGE * j)
             tail[pl.ds(j, EDGE, stride=SUB), :] = rolled(after, -EDGE * j)
         out_ref[unit, pl.ds(0, LANES // SUB)] = wide[...].T.reshape(LANES // SUB, SUB, LANES).astype(jnp.bfloat16)
-        out_ref[unit, pl.ds(LANES // SUB, 2)] = tail[...].T[0:EDGE].reshape(2, SUB, LANES).astype(jnp.bfloat16)
+        out_ref[unit, pl.ds(LANES // SUB, 2)] = tail[:, 0:EDGE].T.reshape(2, SUB, LANES).astype(jnp.bfloat16)
 
 
 def local_place():
@@ -815,11 +815,13 @@
 
 def adam_step(grad_part, first_part, second_part, master_part, hyper_params, clip_scale, keep_decay):
     learn_rate, beta_one, beta_two, weight_decay = (hyper_params[k] for k in range(4))
+    rest, warm = 1.0 - hyper_params, 1.0 - hyper_params ** ADAM_STEP
+    rest_one, rest_two, warm_one, warm_two = rest[1], rest[2], warm[1], warm[2]
     clipped = grad_part * clip_scale
-    moment_one = beta_one * first_part + (1.0 - beta_one) * clipped
-    moment_two = beta_two * second_part + (1.0 - beta_two) * (clipped * clipped)
-    m_hat = moment_one / (1.0 - beta_one ** ADAM_STEP)
-    v_hat = moment_two / (1.0 - beta_two ** ADAM_STEP)
+    moment_one = beta_one * first_part + rest_one * clipped
+    moment_two = beta_two * second_part + rest_two * (clipped * clipped)
+    m_hat = moment_one / warm_one
+    v_hat = moment_two / warm_two
     direction = m_hat / (jnp.sqrt(v_hat) + ADAM_EPS) + jnp.where(keep_decay, weight_decay * master_part, 0.0)
     new_master = master_part - learn_rate * direction
     return moment_one, moment_two, new_master

time: 501 us -> 493 us (0.984)
  Pallas kernels: 469 us -> 463 us
  between operations: 7.2 us -> 2.04 us
    pallas_call x1, Pallas kernels: 282 us -> 276 us  [reduce_scatter(): pl.pallas_call(reduce_kernel, name='reduce_scatter', out_shape=[jax.Shape...]
where the time goes in v4:
time: 493 us
  Pallas kernels  463 us (94%)
  other arithmetic  13.2 us (3%)
  local copies, waits for them, and re-layouts  9.07 us (2%)
    pallas_call x1, Pallas kernels, reduce_scatter(): pl.pallas_call(reduce_kernel, name='reduce_scatter', out_shape=[jax.Shape...  276 us
    pallas_call x1, Pallas kernels, all_gather(): pl.pallas_call(gather_kernel, name='all_gather', out_shape=jax.ShapeDtype...  151 us
    pallas_call x1, Pallas kernels, unpack(): pl.pallas_call(unpack_kernel, name='unpack', out_shape=[jax.ShapeDtypeStr...  22.9 us
    sub x1, other arithmetic, adam_step(): new_master = master_part - learn_rate * direction  11.9 us
  transfers between devices with their start and end apart: 1, of which 1 were waited for; matrix products, arithmetic and copies ran while one was open for 0% of the time, Pallas kernels for 0%

profile of v4, /device:TPU:3, one launch (start us, length us, event | category | flops | bytes accessed | tf_op | source)
XLA Modules:
  0.0 492.8 jit_solution(13981520949507175520)
XLA Ops:
  0.6 0.7 broadcast_subtract_fusion
  1.3 1.4 fusion.2
  2.7 0.7 copy.27
  3.4 0.9 reshape.123
  4.4 0.7 pad_maximum_fusion
  5.1 276.3 %reduce_scatter.1 = (f32[30,18,8,128]{3,2,1,0:T(8,128)}, f32[1]{0:T(128)}) custom-call(bf16[500,18,8,128]{3,2,1,0:T(8,128)(2,1)} %bitcast.121, bf16[6,4,18,8,128]{4,3,2,1,0:T(8,128)(2,1)} %bitcast.127, bf16[6,2,18,8,128]{4,3,2,1,0:T(8,128)(2,1)} %bitcast.130, bf16[6,2,18,8,128]{4,3,2,1,0:T(8,128)(2,1)} %bitcast.131, bf16[24,18,8,128]{3,2,1,0:T(8,128)(2,1)} %bitcast.128, ...), custom_call_target="tpu_custom_call" | custom-call | tf_op jit(solution)/shard_map/reduce_scatter/pallas_call | solution.py:461
  282.1 0.0 copy-start.1
  282.1 6.7 %to_flat.1 = f32[4048,128]{1,0:T(8,128)} custom-call(f32[4320,128]{1,0:T(8,128)} %bitcast.126), custom_call_target="tpu_custom_call" | custom-call | tf_op jit(solution)/shard_map/to_flat/pallas_call | solution.py:757
  288.8 0.6 fusion.3
  290.1 0.0 copy-done.1
  290.1 11.9 %multiply_subtract_fusion = (f32[517920]{0:T(1024)S(1)}, f32[517920]{0:T(1024)}, f32[517920]{0:T(1024)}) fusion(f32[517920]{0:T(1024)S(1)} %copy-done.1, f32[]{:T(128)} %bitcast.42, s32[]{:T(128)S(6)} %mul.76, f32[]{:T(128)} %bitcast.41, f32[]{:T(128)} %bitcast.38, f32[]{:T(128)} %bitcast, f32[]{:T(128)} %bitcast.37, f32[518144]{0:T(1024)} %bitcast.122, ...), kind=kLoop, calls=%fused_computation.2 | loop fusion | flops 9840480 | bytes 14501800 | tf_op jit(solution)/shard_map/sub | solution.py:826
  301.9 0.1 slice.58
  302.0 4.9 collective-permute-start
  306.9 1.4 pad_bitcast_fusion.in_ref
  308.4 0.0 copy-done
  308.4 0.5 collective-permute-done
  308.8 0.7 copy-done.2
  309.5 6.5 %to_tiles.1.a_ref = bf16[30,18,8,128]{3,2,1,0:T(8,128)(2,1)} custom-call(f32[288,128]{1,0:T(8,128)} %bitcast.132, f32[4048,128]{1,0:T(8,128)} %pad_bitcast_fusion.in_ref), custom_call_target="tpu_custom_call" | custom-call | tf_op jit(solution)/shard_map/to_tiles/pallas_call | solution.py:806
  316.0 150.8 %all_gather.1 = bf16[4,2,2,2,29,18,8,128]{7,6,5,4,3,2,1,0:T(8,128)(2,1)} custom-call(bf16[30,18,8,128]{3,2,1,0:T(8,128)(2,1)} %to_tiles.1.a_ref), custom_call_target="tpu_custom_call" | custom-call | tf_op jit(solution)/shard_map/all_gather/pallas_call | solution.py:582
  466.7 22.9 %unpack.1 = (bf16[500,18,8,128]{3,2,1,0:T(8,128)(2,1)}, bf16[6,4,18,8,128]{4,3,2,1,0:T(8,128)(2,1)}, bf16[6,2,18,8,128]{4,3,2,1,0:T(8,128)(2,1)}, bf16[6,2,18,8,...) custom-call(bf16[32,29,18,8,128]{4,3,2,1,0:T(8,128)(2,1)} %bitcast.120), custom_call_target="tpu_custom_call" | custom-call | tf_op jit(solution)/shard_map/unpack/pallas_call | solution.py:121
  489.6 0.9 slice.54
  490.5 1.0 slice.55
  491.5 0.6 slice.59
  492.1 0.7 reshape.137
  (3 shorter events, 0.0 us)
Async XLA Ops:
  282.1 8.0 %copy-start.1 = (f32[517920]{0:T(1024)S(1)}, f32[517920]{0:T(1024)}, u32[]{:S(2)}) copy-start(f32[517920]{0:T(1024)} %param.26) | copy-start | bytes 6215044
  301.9 6.4 %copy-start = (f32[517920]{0:T(1024)}, f32[517920]{0:T(1024)S(1)}, u32[]{:S(2)}) copy-start(f32[517920]{0:T(1024)S(1)} %get-tuple-element.35) | copy-start | bytes 6215044
  302.0 6.8 %collective-permute-start = (f32[36864]{0:T(1024)S(1)}, f32[36864]{0:T(1024)S(1)}, u32[]{:S(2)}, u32[]{:S(2)}) collective-permute-start(f32[36864]{0:T(1024)S(1)} %slice.58), channel_id=1, source_target_pairs={{0,1},{1,2},{2,3},{3,4},{4,5},{5,6},{6,7},{7,8},{8,9},{9,10},{10,1... | collective-permute-start | bytes 442376 | tf_op jit(solution)/shard_map/ppermute | solution.py:860
  308.8 0.7 copy-start.2

commit v5 on v4

--- a/solution.py
+++ b/solution.py
@@ -165,6 +165,7 @@
 
 COLORS = range(4)
 OUTER = 8
+NORM_SLOTS = 13
 DEPTH = 3
 AHEAD = 1
 PHASE = (0, 1, 3, 5)
@@ -387,7 +388,7 @@
     for t in range(DEPTH):
         start_in(t)
     z_peers = Line().peers
-    plane = [index_of(z, y, x, 1 - c), index_of(z, y, 1 - x, c), index_of(z, y, 1 - x, 1 - c), index_of(z, 1 - y, x, c), index_of(z, 1 - y, x, 1 - c)]
+    plane = [index_of(z, (y + k // LINE) % 2, (x + k // 2) % 2, (c + k) % 2) for k in range(1, SUB)]
     greet(plane + z_peers)
     first = first_unit(me)
     begin = first - jnp.minimum(first, END - COVER)
@@ -416,7 +417,7 @@
     sems = Sems(send_n, recv_n)
     sent, used = [], 0
     norm_buf[0] = acc
-    for peers in (z_peers, plane[:3], plane[3:4]):
+    for peers in (z_peers, plane):
         copies = [sems.copy(norm_buf.at[used], norm_buf.at[used + 1 + k], peer) for k, peer in enumerate(peers)]
         start_all(copies)
         recv_all(copies)
@@ -467,10 +468,10 @@
         scratch_shapes=[
             pltpu.VMEM((DEPTH, LINE, 2, 2, 2, most) + TAIL, jnp.bfloat16),
             pltpu.VMEM((PHASE[2] + 1, most, LINE, 2) + TAIL, jnp.float32),
-            pltpu.VMEM((11, SUB, LANES), jnp.float32),
+            pltpu.VMEM((NORM_SLOTS, SUB, LANES), jnp.float32),
             dma((DEPTH,)),
-            dma((OUTER,)),
-            dma((OUTER,)),
+            dma((NORM_SLOTS,)),
+            dma((NORM_SLOTS,)),
         ] + scratch,
         compiler_params=pltpu.CompilerParams(collective_id=0, has_side_effects=True, vmem_limit_bytes=BIG_VMEM),
     )(*tensors)

time: 493 us -> 492 us (level)
  no operation moved by 1% of the time
where the time goes in v5:
time: 492 us
  Pallas kernels  463 us (94%)
  other arithmetic  13.2 us (3%)
  local copies, waits for them, and re-layouts  9.07 us (2%)
    pallas_call x1, Pallas kernels, reduce_scatter(): pl.pallas_call(reduce_kernel, name='reduce_scatter', out_shape=[jax.Shape...  276 us
    pallas_call x1, Pallas kernels, all_gather(): pl.pallas_call(gather_kernel, name='all_gather', out_shape=jax.ShapeDtype...  152 us
    pallas_call x1, Pallas kernels, unpack(): pl.pallas_call(unpack_kernel, name='unpack', out_shape=[jax.ShapeDtypeStr...  22.9 us
    sub x1, other arithmetic, adam_step(): new_master = master_part - learn_rate * direction  11.9 us
  transfers between devices with their start and end apart: 1, of which 1 were waited for; matrix products, arithmetic and copies ran while one was open for 0% of the time, Pallas kernels for 0%

profile of v5, /device:TPU:3, one launch (start us, length us, event | category | flops | bytes accessed | tf_op | source)
XLA Modules:
  0.0 491.7 jit_solution(2282522861799122920)
XLA Ops:
  0.6 0.7 broadcast_subtract_fusion
  1.3 1.4 fusion.2
  2.7 0.7 copy.27
  3.4 0.9 reshape.123
  4.4 0.7 pad_maximum_fusion
  5.1 275.7 %reduce_scatter.1 = (f32[30,18,8,128]{3,2,1,0:T(8,128)}, f32[1]{0:T(128)}) custom-call(bf16[500,18,8,128]{3,2,1,0:T(8,128)(2,1)} %bitcast.121, bf16[6,4,18,8,128]{4,3,2,1,0:T(8,128)(2,1)} %bitcast.127, bf16[6,2,18,8,128]{4,3,2,1,0:T(8,128)(2,1)} %bitcast.130, bf16[6,2,18,8,128]{4,3,2,1,0:T(8,128)(2,1)} %bitcast.131, bf16[24,18,8,128]{3,2,1,0:T(8,128)(2,1)} %bitcast.128, ...), custom_call_target="tpu_custom_call" | custom-call | tf_op jit(solution)/shard_map/reduce_scatter/pallas_call | solution.py:462
  281.4 0.0 copy-start.1
  281.4 6.7 %to_flat.1 = f32[4048,128]{1,0:T(8,128)} custom-call(f32[4320,128]{1,0:T(8,128)} %bitcast.126), custom_call_target="tpu_custom_call" | custom-call | tf_op jit(solution)/shard_map/to_flat/pallas_call | solution.py:758
  288.1 0.6 fusion.3
  289.4 0.0 copy-done.1
  289.4 11.9 %multiply_subtract_fusion = (f32[517920]{0:T(1024)S(1)}, f32[517920]{0:T(1024)}, f32[517920]{0:T(1024)}) fusion(f32[517920]{0:T(1024)S(1)} %copy-done.1, f32[]{:T(128)} %bitcast.42, s32[]{:T(128)S(6)} %mul.76, f32[]{:T(128)} %bitcast.41, f32[]{:T(128)} %bitcast.38, f32[]{:T(128)} %bitcast, f32[]{:T(128)} %bitcast.37, f32[518144]{0:T(1024)} %bitcast.122, ...), kind=kLoop, calls=%fused_computation.2 | loop fusion | flops 9840480 | bytes 14501800 | tf_op jit(solution)/shard_map/sub | solution.py:827
  301.3 0.1 slice.58
  301.4 3.6 collective-permute-start
  305.0 1.4 pad_bitcast_fusion.in_ref
  306.4 0.0 copy-done
  306.4 0.5 collective-permute-done
  306.9 0.7 copy-done.2
  307.5 6.5 %to_tiles.1.a_ref = bf16[30,18,8,128]{3,2,1,0:T(8,128)(2,1)} custom-call(f32[288,128]{1,0:T(8,128)} %bitcast.132, f32[4048,128]{1,0:T(8,128)} %pad_bitcast_fusion.in_ref), custom_call_target="tpu_custom_call" | custom-call | tf_op jit(solution)/shard_map/to_tiles/pallas_call | solution.py:807
  314.0 151.5 %all_gather.1 = bf16[4,2,2,2,29,18,8,128]{7,6,5,4,3,2,1,0:T(8,128)(2,1)} custom-call(bf16[30,18,8,128]{3,2,1,0:T(8,128)(2,1)} %to_tiles.1.a_ref), custom_call_target="tpu_custom_call" | custom-call | tf_op jit(solution)/shard_map/all_gather/pallas_call | solution.py:583
  465.6 22.9 %unpack.1 = (bf16[500,18,8,128]{3,2,1,0:T(8,128)(2,1)}, bf16[6,4,18,8,128]{4,3,2,1,0:T(8,128)(2,1)}, bf16[6,2,18,8,128]{4,3,2,1,0:T(8,128)(2,1)}, bf16[6,2,18,8,...) custom-call(bf16[32,29,18,8,128]{4,3,2,1,0:T(8,128)(2,1)} %bitcast.120), custom_call_target="tpu_custom_call" | custom-call | tf_op jit(solution)/shard_map/unpack/pallas_call | solution.py:121
  488.5 0.9 slice.54
  489.4 1.0 slice.55
  490.4 0.6 slice.59
  491.0 0.7 reshape.137
  (3 shorter events, 0.0 us)
Async XLA Ops:
  281.4 8.0 %copy-start.1 = (f32[517920]{0:T(1024)S(1)}, f32[517920]{0:T(1024)}, u32[]{:S(2)}) copy-start(f32[517920]{0:T(1024)} %param.26) | copy-start | bytes 6215044
  301.3 5.2 %copy-start = (f32[517920]{0:T(1024)}, f32[517920]{0:T(1024)S(1)}, u32[]{:S(2)}) copy-start(f32[517920]{0:T(1024)S(1)} %get-tuple-element.35) | copy-start | bytes 6215044
  301.4 5.5 %collective-permute-start = (f32[36864]{0:T(1024)S(1)}, f32[36864]{0:T(1024)S(1)}, u32[]{:S(2)}, u32[]{:S(2)}) collective-permute-start(f32[36864]{0:T(1024)S(1)} %slice.58), channel_id=1, source_target_pairs={{0,1},{1,2},{2,3},{3,4},{4,5},{5,6},{6,7},{7,8},{8,9},{9,10},{10,1... | collective-permute-start | bytes 442376 | tf_op jit(solution)/shard_map/ppermute | solution.py:861
  306.9 0.7 copy-start.2
